TPU v7x, 32 devices: a whole 2x2x4 slice. The times are simulated.
32 devices in a mesh: tm: 8 (over z, y), coef: 4 (over x, core).
Axes of the slice: x: 2, y: 2, z: 4, core: 2. Of those that a mesh axis runs over, the one named last changes fastest.
Arguments:
- design: bfloat16 [2048, 50176], P('tm', 'coef'), may hold values from -0.0390625 to 0.0390625
- observed: float32 [2048, 128], P('tm'), may hold values from -6 to 6
- slab_counts: int32 [8], P('tm'), may hold values from 128 to 256, as said below
- gap_mask: int32 [2048], P('tm'), may hold values 0 or 1
- filter_taps: float32 [128], replicated, may hold values from -0.5 to 1.2, as said below
- kaula_diag: float32 [50176], P('coef'), may hold values from 0.1 to 1
- precond: float32 [50176], P('coef'), may hold values from 0.3 to 3
Outputs:
- solution: float32 [50176, 128], P(('coef', 'tm'))
- residual: float32 [50176, 128], P(('coef', 'tm'))
Inputs may be any that keep to these rules, and one draw needn't show every extreme that they name: `slab_counts`: every slab holds at most 256 valid epochs, and some slab holds exactly 256. filter_taps[0] lies between 1 and 1.2.
All inputs are finite; a program needn't handle non-finite values. No bound on the sum of `gap_mask` on one device may be relied on, other than what follows from the above.
Results may differ from a plain program's by a relative error of at most 0.0065.
The roundings to bfloat16 on the way count: a program that leaves them out, or rounds other values in their place, can miss the bound.
Values may be sent and summed in bfloat16 or wider, within the bound.
A program may use at most 64 MiB of HBM per device.

v0:
```python
import jax
import jax.numpy as jnp
from jax import lax
from jax.sharding import PartitionSpec as P

ITERS = 2
HIGHEST = lax.Precision.HIGHEST


def toeplitz(pattern, band_len):
    tiled = jnp.tile(pattern, band_len)[: band_len * (2 * band_len - 1)]
    return tiled.reshape(band_len, 2 * band_len - 1)[:, :band_len]


def block_pair(filter_taps):
    band_len = filter_taps.shape[0]
    spacer = jnp.zeros((band_len,), jnp.float32)
    reversed_taps = filter_taps[:0:-1]
    lower = jnp.concatenate([filter_taps[:1], spacer, reversed_taps])
    upper = jnp.concatenate([jnp.zeros((1,), jnp.float32), reversed_taps, spacer])
    return (toeplitz(lower, band_len), toeplitz(upper, band_len))


def forward(values, lower_block, upper_block):
    band_len = lower_block.shape[0]
    blocks = values.reshape(-1, band_len, values.shape[1])
    previous = jnp.concatenate([jnp.zeros_like(blocks[:1]), blocks[:-1]], 0)
    result = jnp.einsum("ij,bjr->bir", lower_block, blocks, precision=HIGHEST)
    result = result + jnp.einsum("ij,bjr->bir", upper_block, previous, precision=HIGHEST)
    return result.reshape(values.shape)


def backward(values, lower_block, upper_block):
    band_len = lower_block.shape[0]
    blocks = values.reshape(-1, band_len, values.shape[1])
    following = jnp.concatenate([blocks[1:], jnp.zeros_like(blocks[:1])], 0)
    result = jnp.einsum("ji,bjr->bir", lower_block, blocks, precision=HIGHEST)
    result = result + jnp.einsum("ji,bjr->bir", upper_block, following, precision=HIGHEST)
    return result.reshape(values.shape)


def shards(design, observed, slab_counts, gap_mask, filter_taps, kaula_diag, precond):
    epoch_rows, coef_rows = design.shape
    columns = observed.shape[1]
    slabs = lax.axis_size("tm")
    epochs = slabs * epoch_rows
    owned_rows = coef_rows // slabs
    owner_index = lax.axis_index("tm")
    lower_block, upper_block = block_pair(filter_taps)
    position = jnp.arange(epoch_rows, dtype=jnp.int32)
    local_weight = ((gap_mask == 1) & (position < slab_counts[0])).astype(jnp.float32)
    packed = jnp.concatenate([observed, local_weight.reshape(-1, columns)], 0)
    gathered = lax.all_gather(packed, "tm", axis=0, tiled=False)
    all_observed = gathered[:, :epoch_rows].reshape(epochs, columns)
    weight = gathered[:, epoch_rows:].reshape(epochs, 1)
    block = lax.all_to_all(design, "tm", split_axis=1, concat_axis=0, tiled=True)

    def weighted(values):
        inner = forward(weight * values, lower_block, upper_block)
        return (weight * backward(inner, lower_block, upper_block)).astype(jnp.bfloat16)

    def transposed(filtered):
        return lax.dot_general(
            block, filtered, (((0,), (0,)), ((), ())), preferred_element_type=jnp.float32
        )

    def summed(scaled, terms):
        partial = jnp.dot(block, scaled.astype(jnp.bfloat16), preferred_element_type=jnp.float32)
        rows = [jnp.sum(term, 0)[None] for term in terms]
        rows.append(jnp.zeros((8 - len(rows), columns), jnp.float32))
        total = lax.psum(jnp.concatenate([partial] + rows, 0), ("tm", "coef"))
        return total[:epochs], [total[epochs + at] for at in range(len(terms))]

    start = owner_index * owned_rows
    kaula_col = lax.dynamic_slice_in_dim(kaula_diag, start, owned_rows, 0)[:, None]
    precond_col = lax.dynamic_slice_in_dim(precond, start, owned_rows, 0)[:, None]
    residual = transposed(weighted(all_observed))
    solution = jnp.zeros_like(residual)
    for iteration in range(ITERS):
        scaled = precond_col * residual
        terms = [residual * scaled, kaula_col * scaled * scaled]
        if iteration == 0:
            slab_values, (norm_now, ridge) = summed(scaled, terms)
            direction = scaled
        else:
            terms.append(kaula_col * scaled * direction)
            fresh, (norm_next, own_ridge, cross) = summed(scaled, terms)
            ratio = norm_next / norm_now
            slab_values = fresh + ratio * slab_values
            ridge = own_ridge + ratio * (2.0 * cross + ratio * ridge)
            direction = scaled + ratio * direction
            norm_now = norm_next
        filtered = weighted(slab_values)
        curvature = ridge + jnp.sum(slab_values * filtered.astype(jnp.float32), 0)
        step_len = norm_now / curvature
        image = transposed(filtered) + kaula_col * direction
        solution = solution + step_len * direction
        residual = residual - step_len * image
    return (solution, residual)


def solution(mesh):
    placed = (P("tm", "coef"), P("tm", None), P("tm"), P("tm"), P(), P("coef"), P("coef"))
    return jax.shard_map(
        shards,
        mesh=mesh,
        in_specs=placed,
        out_specs=(P(("coef", "tm"), None), P(("coef", "tm"), None)),
        check_vma=False,
    )
```

profile of v0, /device:TPU:0, one launch (start us, length us, event | category | flops | bytes accessed | tf_op | source)
XLA Modules:
  0.0 508.5 jit_solution(15422720378014263486)
XLA Ops:
  7.2 9.5 %copy.77 = bf16[256,12544]{0,1:T(8,128)(2,1)} copy(bf16[256,12544]{1,0:T(8,128)(2,1)} %param.7) | data formatting | bytes 12845056 | tf_op args[0]
  16.7 7.4 %all-to-all-start = ((bf16[256,8,1568]{0,2,1:T(8,128)(2,1)}), bf16[256,8,1568]{0,2,1:T(8,128)(2,1)}, u32[]{:S(2)}, u32[]{:S(2)}) async-start(bf16[256,8,1568]{0,2,1:T(8,128)(2,1)} %bitcast.147), calls=%async_computation | async-start | bytes 12845056 | tf_op jit(solution)/shard_map/all_to_all | solution.py:56
  24.9 0.7 maximum_bitcast_fusion
  25.6 0.8 dynamic_slice.7
  26.4 0.8 dynamic_slice.6
  27.6 0.3 reshape.76
  28.0 0.3 reshape.78
  28.3 150.4 %all-gather.4.cloned.1.call-done = f32[8,258,128]{2,1,0:T(8,128)} async-done(((f32[1,258,128]{2,1,0:T(8,128)}), f32[8,258,128]{2,1,0:T(8,128)}) %all-gather.4.cloned.1.call-update) | async-done | bytes 1056784 | tf_op jit(solution)/shard_map/all_gather | solution.py:53
  178.8 1.3 slice.97
  180.1 0.3 copy.124
  180.5 0.8 slice.96
  181.3 0.3 copy.71
  181.6 2.1 fusion.19
  183.8 1.7 fusion.8
  185.5 1.1 fusion.42
  186.6 1.1 fusion.10
  187.7 3.7 copy.127
  191.4 1.9 fusion.27
  193.4 0.8 copy-done
  194.1 1.2 convolution_bitcast_fusion.4
  195.6 1.2 concatenate.38
  197.1 128.1 %all-reduce.9.cloned.1.call-done = f32[2056,128]{0,1:T(8,128)} async-done(((f32[2056,128]{0,1:T(8,128)}), f32[2056,128]{0,1:T(8,128)}) %all-reduce.9.cloned.1.call-update) | async-done | bytes 1052688 | tf_op jit(solution)/shard_map/psum | solution.py:71
  325.2 1.4 slice_multiply_fusion
  326.7 0.3 copy.82
  327.1 1.0 fusion.14
  328.1 1.7 fusion.7
  329.8 1.1 fusion.41
  330.9 2.0 fusion.18
  332.8 1.3 copy.120
  334.2 2.1 multiply_reduce_fusion.1
  336.3 0.8 copy.89
  337.3 5.3 %fusion.29 = (f32[128]{0:T(128)S(1)}, f32[128]{0:T(128)S(1)}, f32[128]{0:T(128)S(1)}, f32[1568,128]{1,0:T(8,128)S(1)}) fusion(f32[1568,128]{1,0:T(8,128)} %copy-done.2, f32[1568]{0:T(1024)} %copy-done.10, f32[1568]{0:T(1024)S(1)} %dynamic_slice.6, bf16[2048,1568]{0,1:T(8,128)(2,1)} %bitcast.142, bf16[2048,128]{1,0:T(8,128)(2,1)} %bitcast.166, ...), kind=kOutput, calls=%fused_computation.58 | convolution fusion | flops 824692352 | bytes 8567040 | tf_op jit(solution)/shard_map/dot_general | solution.py:63
  342.6 2.2 convolution_bitcast_fusion.3
  345.2 2.4 concatenate.41
  347.7 130.8 %all-reduce.11.cloned.1.call-done = f32[2056,128]{0,1:T(8,128)} async-done(((f32[2056,128]{0,1:T(8,128)}), f32[2056,128]{0,1:T(8,128)}) %all-reduce.11.cloned.1.call-update) | async-done | bytes 1052688 | tf_op jit(solution)/shard_map/psum | solution.py:71
  478.5 0.9 fusion.44
  479.4 1.4 broadcast_multiply_fusion
  480.9 1.0 fusion.11
  481.9 1.1 slice.114
  482.9 1.5 copy.94
  484.4 1.7 fusion.6
  486.2 1.1 fusion.40
  487.3 2.2 fusion.17
  489.5 2.6 copy.123
  492.1 1.8 multiply_reduce_fusion
  494.0 1.2 fusion.39
  495.3 1.2 fusion.26
  496.4 5.5 %fusion.5 = f32[1568,128]{1,0:T(8,128)} fusion(f32[1568,128]{1,0:T(8,128)S(1)} %copy-done.5, bf16[2048,1568]{0,1:T(8,128)(2,1)} %bitcast.143, bf16[2048,128]{1,0:T(8,128)(2,1)S(1)} %bitcast.155, f32[1568,128]{1,0:T(8,128)S(1)} %copy-done.3, f32[128]{0:T(128)S(1)} %fusion.44, f32[128]{0:T(128)S(1)} %fusion.39, f32[1568]{0:T(1024)S(1)} %copy-done.11, ...), kind=kOutput, calls=%fused_computation.10 | convolution fusion | flops 823689216 | bytes 9368832 | tf_op jit(solution)/shard_map/dot_general | solution.py:63
  (63 shorter events, 1.9 us)
Async XLA Ops:
  16.7 8.1 %copy-start.14 = (s32[256]{0:T(256)S(1)}, s32[256]{0:T(256)}, u32[]{:S(2)}) copy-start(s32[256]{0:T(256)} %param.10) | copy-start | bytes 3076
  16.7 8.2 %copy-start.9 = (f32[256,128]{1,0:T(8,128)S(1)}, f32[256,128]{1,0:T(8,128)}, u32[]{:S(2)}) copy-start(f32[256,128]{1,0:T(8,128)} %param.8) | copy-start | bytes 393220
  16.7 10.5 %copy-start.15 = (f32[128]{0:T(128)S(1)}, f32[128]{0:T(128)}, u32[]{:S(2)}) copy-start(f32[128]{0:T(128)} %param.11) | copy-start | bytes 1540
  16.7 171.0 %all-to-all-start = ((bf16[256,8,1568]{0,2,1:T(8,128)(2,1)}), bf16[256,8,1568]{0,2,1:T(8,128)(2,1)}, u32[]{:S(2)}, u32[]{:S(2)}) async-start(bf16[256,8,1568]{0,2,1:T(8,128)(2,1)} %bitcast.147), calls=%async_computation | async-start | bytes 12845056 | tf_op jit(solution)/shard_map/all_to_all | solution.py:56
  24.1 154.6 %all-gather.4.cloned.1.call-start = ((), (), s32[]{:S(2)}) async-start(), calls=%async_computation.3 | async-start | bytes 1216512 | tf_op jit(solution)/shard_map/all_gather | solution.py:53
  25.6 299.7 %all-reduce.9.cloned.1.call-start = ((), (), s32[]{:S(2)}) async-start(), calls=%async_computation.1 | async-start | bytes 2228224 | tf_op jit(solution)/shard_map/psum | solution.py:71
  26.4 165.0 %copy-start.10 = (f32[1568]{0:T(1024)}, f32[1568]{0:T(1024)S(1)}, u32[]{:S(2)}) copy-start(f32[1568]{0:T(1024)S(1)} %dynamic_slice.7) | copy-start | bytes 18820
  27.9 157.6 %copy-start.6 = (f32[128,255]{1,0:T(8,128)}, f32[128,255]{1,0:T(8,128)S(1)}, u32[]{:S(2)}) copy-start(f32[128,255]{1,0:T(8,128)S(1)} %reshape.76) | copy-start | bytes 391684
  191.4 2.7 copy-start
  193.4 2.0 copy-start.2
  195.4 131.7 %copy-start.7 = (f32[128,255]{1,0:T(8,128)S(1)}, f32[128,255]{1,0:T(8,128)}, u32[]{:S(2)}) copy-start(f32[128,255]{1,0:T(8,128)} %copy-done.6) | copy-start | bytes 391684
  196.9 281.6 %all-reduce.11.cloned.1.call-start = ((), (), s32[]{:S(2)}) async-start(), calls=%async_computation.2 | async-start | bytes 2228224 | tf_op jit(solution)/shard_map/psum | solution.py:71
  325.2 1.8 copy-start.1
  334.2 8.5 %slice-start = ((s8[6422528]{0:T(1024)(128)(4,1)}), s8[2228224]{0:T(1024)(128)(4,1)S(1)}, s32[]{:S(2)}) async-start(s8[6422528]{0:T(1024)(128)(4,1)} %bitcast.144), calls=%async_computation.4 | async-start | bytes 4456448
  337.3 5.3 %copy-start.12 = (f32[128]{0:T(128)}, f32[128]{0:T(128)S(1)}, u32[]{:S(2)}) copy-start(f32[128]{0:T(128)S(1)} %fusion.38) | copy-start | bytes 1540
  337.3 5.4 %slice-start.1 = ((s8[6422528]{0:T(1024)(128)(4,1)}), s8[4194304]{0:T(1024)(128)(4,1)S(1)}, s32[]{:S(2)}) async-start(s8[6422528]{0:T(1024)(128)(4,1)} %bitcast.144), calls=%async_computation.5 | async-start | bytes 8388608
  342.6 2.3 copy-start.4
  344.9 135.9 %copy-start.8 = (f32[128,255]{1,0:T(8,128)S(1)}, f32[128,255]{1,0:T(8,128)}, u32[]{:S(2)}) copy-start(f32[128,255]{1,0:T(8,128)} %copy-done.6) | copy-start | bytes 391684
  486.2 9.1 %copy-start.3 = (f32[1568,128]{1,0:T(8,128)S(1)}, f32[1568,128]{1,0:T(8,128)}, u32[]{:S(2)}) copy-start(f32[1568,128]{1,0:T(8,128)} %copy-done.2) | copy-start | bytes 2408452
  486.2 9.1 %copy-start.5 = (f32[1568,128]{1,0:T(8,128)S(1)}, f32[1568,128]{1,0:T(8,128)}, u32[]{:S(2)}) copy-start(f32[1568,128]{1,0:T(8,128)} %copy-done.4) | copy-start | bytes 2408452
  486.2 9.1 %copy-start.13 = (f32[128]{0:T(128)S(1)}, f32[128]{0:T(128)}, u32[]{:S(2)}) copy-start(f32[128]{0:T(128)} %copy-done.12) | copy-start | bytes 1540
  487.3 9.1 %copy-start.11 = (f32[1568]{0:T(1024)S(1)}, f32[1568]{0:T(1024)}, u32[]{:S(2)}) copy-start(f32[1568]{0:T(1024)} %copy-done.10) | copy-start | bytes 18820
Sparse Core Ops, SparseCore 0:
  27.7 151.0 all-gather.3
  197.0 128.1 all-reduce.8
  347.8 130.6 all-reduce.10
where the time goes:
time: 510 us; the launch traced here: 509 us
  waiting for transfers between devices  409 us (80%)
  matrix products  33.9 us (7%)
  local copies, waits for them, and re-layouts  31.5 us (6%)
  between operations  14.8 us (3%)
  other arithmetic  11.1 us (2%)
  starting transfers between devices  7.75 us (2%)
    psum x2, waiting for transfers between devices, summed(): total = lax.psum(jnp.concatenate([partial] + rows, 0), ('tm', 'coef'))  259 us
    all_gather x1, waiting for transfers between devices, shards(): gathered = lax.all_gather(packed, 'tm', axis=0, tiled=False)  150 us
    dot_general x3, matrix products, transposed(): lax.dot_general(block, filtered, (((0,), (0,)), ((), ())), preferred_elem...  12.8 us
    unnamed x41, local copies, waits for them, and re-layouts  10.8 us
  transfers between devices with their start and end apart: 4, of which 3 were waited for; matrix products, arithmetic and copies ran while one was open for 2% of the time, Pallas kernels for 0%

commit v1 on v0

--- a/solution.py
+++ b/solution.py
@@ -1,6 +1,10 @@
+import functools
+
 import jax
 import jax.numpy as jnp
 from jax import lax
+from jax.experimental import pallas as pl
+from jax.experimental.pallas import tpu as pltpu
 from jax.sharding import PartitionSpec as P
 
 ITERS = 2
@@ -39,7 +43,7 @@
     return result.reshape(values.shape)
 
 
-def shards(design, observed, slab_counts, gap_mask, filter_taps, kaula_diag, precond):
+def general_shards(design, observed, slab_counts, gap_mask, filter_taps, kaula_diag, precond):
     epoch_rows, coef_rows = design.shape
     columns = observed.shape[1]
     slabs = lax.axis_size("tm")
@@ -99,6 +103,398 @@
     return (solution, residual)
 
 
+LANES = 128
+MESH = pl.DeviceIdType.MESH
+
+
+class Plan:
+    def __init__(self, slabs, coefs, epoch_rows, coef_rows, columns):
+        self.slabs, self.coefs, self.epoch_rows, self.columns = slabs, coefs, epoch_rows, columns
+        self.owned = coef_rows // slabs
+        last = coef_rows // LANES
+        tiles = 0
+        for owner in range(slabs):
+            first = owner * self.owned // LANES
+            tiles = max(tiles, (owner * self.owned + self.owned - 1) // LANES - first + 1)
+        self.width = tiles * LANES
+        self.last_tile = last - tiles
+        self.across = coefs // 2
+        self.chips = slabs * self.across
+        self.group = columns // self.chips
+        self.blocks = slabs * epoch_rows // LANES
+        self.half = slabs * epoch_rows // 2
+        self.message = self.half + LANES
+
+    def first_tile(self, owner):
+        return lax.min(lax.div(owner * self.owned, LANES), self.last_tile)
+
+
+def fits(slabs, coefs, epoch_rows, coef_rows, columns, taps):
+    power = slabs & (slabs - 1) == 0
+    if not power or slabs < 2 or coefs % 2 or coef_rows % LANES or coef_rows % slabs or epoch_rows % LANES:
+        return False
+    return taps == LANES and columns == LANES and columns == 8 * slabs * coefs // 2
+
+
+def flipped(index, bits, count):
+    result, weight = 0, 1
+    while weight < count:
+        bit = lax.rem(lax.div(index, weight), 2)
+        result = result + weight * (1 - bit if bits & weight else bit)
+        weight *= 2
+    return result
+
+
+def pieces(values):
+    high = values.astype(jnp.bfloat16).astype(jnp.float32)
+    rest = values - high
+    middle = rest.astype(jnp.bfloat16).astype(jnp.float32)
+    low = (rest - middle).astype(jnp.bfloat16).astype(jnp.float32)
+    return high + pltpu.roll(middle, 8, 1) + pltpu.roll(low, 16, 1)
+
+
+def joined(values, at):
+    lane = lax.broadcasted_iota(jnp.int32, values.shape, 1)
+    taken = (lane % 8 == at) & (lane < 24)
+    return jnp.sum(jnp.where(taken, values, 0.0), 1, keepdims=True)
+
+
+def in_lanes(terms, rows):
+    lane = lax.broadcasted_iota(jnp.int32, (rows, LANES), 1)
+    result = jnp.zeros((rows, LANES), jnp.float32)
+    for at, term in enumerate(terms):
+        result = jnp.where(lane == at, term, result)
+    return result
+
+
+def product(left, right, contract, precision=None):
+    return lax.dot_general(
+        left, right, ((contract[0], contract[1]), ((), ())),
+        precision=precision, preferred_element_type=jnp.float32,
+    )
+
+
+NN = ((1,), (0,))
+NT = ((1,), (1,))
+
+
+def fused(plan, design, observed, gap, counts, taps, kaula, precond, solution_out, residual_out,
+          block, shown, seen, sums, sent, received, total, whole, folded, filtered, gathered, folded_in,
+          resid, direc, scal, solut, image, first_values,
+          own_sem, block_send, block_recv, show_send, show_recv, pair_send, pair_recv,
+          fold_send, fold_recv, whole_send, whole_recv, gather_send, gather_recv, relay_send, relay_recv):
+    slabs, chips, group, rows = plan.slabs, plan.chips, plan.group, plan.epoch_rows
+    half_slabs = slabs // 2
+    slab, coef = lax.axis_index("tm"), lax.axis_index("coef")
+    across, core = lax.div(coef, 2), lax.rem(coef, 2)
+    chip = slab * plan.across + across
+
+    def device(at):
+        return {"tm": lax.div(at, plan.across), "coef": 2 * lax.rem(at, plan.across) + core}
+
+    partner = {"tm": slab, "coef": 2 * across + 1 - core}
+
+    def other(step):
+        return lax.rem(chip + step, chips)
+
+    def remote(src, dst, send, recv, target):
+        return pltpu.make_async_remote_copy(
+            src_ref=src, dst_ref=dst, send_sem=send, recv_sem=recv, device_id=target, device_id_type=MESH
+        )
+
+    barrier = pltpu.get_barrier_semaphore()
+    for step in range(1, chips):
+        pl.semaphore_signal(barrier, inc=1, device_id=device(other(step)), device_id_type=MESH)
+    pl.semaphore_signal(barrier, inc=1, device_id=partner, device_id_type=MESH)
+
+    place = lax.broadcasted_iota(jnp.int32, (1, rows), 1)
+    weight_row = jnp.where((gap[...] == 1) & (place < counts[0]), 1.0, 0.0)
+    turned = observed[...].T * weight_row
+    shown[:, :group, :] = turned.reshape(chips, group, rows)
+    shown[:, group:, :] = jnp.broadcast_to(weight_row[None], (chips, group, rows))
+    seen[slab] = shown[chip]
+
+    first = plan.first_tile(slab)
+    cut = plan.width // LANES // 2 * LANES
+    parts = ((0, cut), (cut, plan.width - cut))
+
+    def block_copy(bits, part):
+        peer = flipped(slab, bits, slabs)
+        low, size = parts[part]
+        src = design.at[:, pl.ds(pl.multiple_of(plan.first_tile(peer) * LANES + low, LANES), size)]
+        dst = block.at[slab, :, pl.ds(low, size)]
+        return remote(src, dst, block_send.at[part, peer], block_recv.at[part, slab], {"tm": peer, "coef": coef})
+
+    def block_arrival(bits, part):
+        peer = flipped(slab, bits, slabs)
+        low, size = parts[part]
+        dst = block.at[peer, :, pl.ds(low, size)]
+        return remote(dst, dst, block_send.at[part, peer], block_recv.at[part, peer], {"tm": peer, "coef": coef})
+
+    def show_copy(bits):
+        peer = flipped(slab, bits, slabs)
+        src = shown.at[peer * plan.across + across]
+        return remote(src, seen.at[slab], show_send.at[peer], show_recv.at[slab], {"tm": peer, "coef": coef})
+
+    def show_arrival(bits):
+        peer = flipped(slab, bits, slabs)
+        return remote(seen.at[peer], seen.at[peer], show_send.at[peer], show_recv.at[peer], {"tm": peer, "coef": coef})
+
+    own = pltpu.make_async_copy(
+        design.at[:, pl.ds(pl.multiple_of(first * LANES, LANES), plan.width)], block.at[slab], own_sem
+    )
+    own.start()
+    pl.semaphore_wait(barrier, chips)
+    for bits in range(1, slabs):
+        show_copy(bits).start()
+    for bits in range(1, slabs):
+        block_copy(bits, 0).start()
+
+    base = jnp.concatenate([taps[...], jnp.zeros((1, LANES), jnp.float32)], 1)
+    shifted = pltpu.roll(jnp.broadcast_to(base, (LANES, 2 * LANES)), 0, 1, stride=1, stride_axis=0)
+    lower, upper = shifted[:, :LANES], shifted[:, LANES:]
+    blank = jnp.zeros((group, LANES), jnp.float32)
+
+    for bits in range(1, slabs):
+        show_arrival(bits).wait_recv()
+
+    def stack(ref, low):
+        return jnp.concatenate(
+            [ref[at, low:low + group, j * LANES:(j + 1) * LANES] for at in range(slabs) for j in range(rows // LANES)], 0
+        )
+
+    weight = stack(seen, group)
+
+    def weighted(values):
+        entering = weight * values
+        before = jnp.concatenate([blank, entering[:-group]], 0)
+        inner = product(entering, lower, NN, lax.Precision.HIGHEST) + product(before, upper, NN, lax.Precision.HIGHEST)
+        after = jnp.concatenate([inner[group:], blank], 0)
+        outer = product(inner, lower, NT, lax.Precision.HIGHEST) + product(after, upper, NT, lax.Precision.HIGHEST)
+        return (weight * outer).astype(jnp.bfloat16)
+
+    def gather_start(phase, values, terms):
+        wide = values.astype(jnp.float32)
+        for half in range(2):
+            for j in range(plan.blocks // 2):
+                low = (half * (plan.blocks // 2) + j) * group
+                folded[half, :, j * LANES:(j + 1) * LANES] = wide[low:low + group]
+            folded[half, :, plan.half:] = pieces(in_lanes(terms, group))
+        gathered[phase, core, chip] = folded[core].astype(jnp.bfloat16)
+
+        def send(step, carry):
+            to = other(step)
+            here = gathered.at[phase, core, chip]
+            remote(here, here, gather_send.at[phase, to], gather_recv.at[phase, chip], device(to)).start()
+            return carry
+
+        lax.fori_loop(1, chips, send, 0)
+
+    def gather_finish(phase):
+        def arrive(step, carry):
+            at = other(step)
+            here = gathered.at[phase, core, at]
+            remote(here, here, gather_send.at[phase, at], gather_recv.at[phase, at], device(at)).wait_recv()
+            return carry
+
+        lax.fori_loop(1, chips, arrive, 0)
+        mine, theirs = gathered.at[phase, core], gathered.at[phase, 1 - core]
+        remote(mine, mine, relay_send.at[phase], relay_recv.at[phase], partner).start()
+        remote(theirs, theirs, relay_send.at[phase], relay_recv.at[phase], partner).wait_recv()
+        for half in range(2):
+            for j in range(half_slabs):
+                values = gathered[phase, half, :, :, j * rows:(j + 1) * rows].astype(jnp.float32)
+                filtered[half * half_slabs + j] = values.reshape(plan.columns, rows).astype(jnp.bfloat16)
+        terms = gathered[phase, 0, :, :, plan.half:].astype(jnp.float32).reshape(plan.columns, LANES)
+        return joined(terms, 0), joined(terms, 1)
+
+    gather_start(0, weighted(stack(seen, 0)), [])
+    for bits in range(1, slabs):
+        block_copy(bits, 1).start()
+
+    spread = pl.ds(pl.multiple_of(first * LANES, LANES), plan.width)
+    ridge_row = kaula[:, spread]
+    lane = lax.broadcasted_iota(jnp.int32, (1, plan.width), 1) + (first * LANES - slab * plan.owned)
+    scale_row = jnp.where((lane >= 0) & (lane < plan.owned), precond[:, spread], 0.0)
+
+    gather_finish(0)
+    own.wait()
+    resid[...] = product(filtered[slab], block[slab], NN)
+    for bits in range(1, slabs):
+        for part in range(2):
+            block_arrival(bits, part).wait_recv()
+        peer = flipped(slab, bits, slabs)
+        resid[...] += product(filtered[peer], block[peer], NN)
+
+    def summed(turn, values, terms):
+        low = values.astype(jnp.bfloat16)
+
+        def one(half):
+            def body(at, carry):
+                sums[turn, half, at] = product(low, block[half * half_slabs + at], NT)
+                return carry
+
+            lax.fori_loop(0, half_slabs, body, 0)
+
+        one(0)
+        one(1)
+        scalars = in_lanes(terms, plan.columns)
+        for half in range(2):
+            sums[turn, half, half_slabs, :, :LANES] = scalars
+        remote(sums.at[turn, 1 - core], received.at[turn], pair_send.at[turn], pair_recv.at[turn], partner).start()
+        remote(sums.at[turn, 1 - core], received.at[turn], pair_send.at[turn], pair_recv.at[turn], partner).wait_recv()
+        for at in range(half_slabs):
+            values = (sums[turn, core, at] + received[turn, at]).reshape(chips, group, rows)
+            total[:, :, at * rows:(at + 1) * rows] = values
+            sent[turn, :, :, at * rows:(at + 1) * rows] = values.astype(jnp.bfloat16)
+        scalars = sums[turn, core, half_slabs, :, :LANES] + received[turn, half_slabs, :, :LANES]
+        total[:, :, plan.half:] = scalars.reshape(chips, group, LANES)
+        sent[turn, :, :, plan.half:] = pieces(scalars).reshape(chips, group, LANES).astype(jnp.bfloat16)
+
+        def send(step, carry):
+            to = other(step)
+            remote(sent.at[turn, to], folded_in.at[turn, chip], fold_send.at[turn, to], fold_recv.at[turn, chip], device(to)).start()
+            return carry
+
+        lax.fori_loop(1, chips, send, 0)
+
+        def arrive(step, carry):
+            at = other(step)
+            here = folded_in.at[turn, at]
+            remote(here, here, fold_send.at[turn, at], fold_recv.at[turn, at], device(at)).wait_recv()
+            return carry + folded_in[turn, at].astype(jnp.float32)
+
+        whole[turn, core] = lax.fori_loop(1, chips, arrive, total[chip])
+        mine, theirs = whole.at[turn, core], whole.at[turn, 1 - core]
+        remote(mine, mine, whole_send.at[turn], whole_recv.at[turn], partner).start()
+        remote(theirs, theirs, whole_send.at[turn], whole_recv.at[turn], partner).wait_recv()
+        values = jnp.concatenate(
+            [whole[turn, half, :, j * LANES:(j + 1) * LANES] for half in range(2) for j in range(plan.blocks // 2)], 0
+        )
+        terms = whole[turn, 0, :, plan.half:]
+        return values, joined(terms, 0), joined(terms, 1), joined(terms, 2)
+
+    def inner(left, right):
+        together = (left * right).reshape(plan.blocks, group, LANES)
+        return jnp.sum(jnp.sum(together, 0), 1, keepdims=True)
+
+    def transposed():
+        image[...] = product(filtered[0], block[0], NN)
+
+        def body(at, carry):
+            image[...] += product(filtered[at], block[at], NN)
+            return carry
+
+        lax.fori_loop(1, slabs, body, 0)
+
+    def over(terms):
+        return jnp.sum(terms, 1, keepdims=True)
+
+    direc[...] = scale_row * resid[...]
+    ridged = ridge_row * direc[...]
+    terms = [over(resid[...] * direc[...]), over(ridged * direc[...])]
+    values, norm, ridge, _ = summed(0, direc[...], terms)
+    first_values[...] = values
+    kept = weighted(values)
+    step_len = norm / (ridge + inner(values, kept.astype(jnp.float32)))
+    gather_start(1, kept, [step_len])
+    step_col, _ = gather_finish(1)
+    transposed()
+    resid[...] = resid[...] - step_col * (image[...] + ridge_row * direc[...])
+    solut[...] = step_col * direc[...]
+    scal[...] = scale_row * resid[...]
+    ridged = ridge_row * scal[...]
+    terms = [over(resid[...] * scal[...]), over(ridged * scal[...]), over(ridged * direc[...])]
+    fresh, norm_next, own_ridge, cross = summed(1, scal[...], terms)
+    ratio = norm_next / norm
+    ridge = own_ridge + ratio * (2.0 * cross + ratio * ridge)
+    values = fresh + jnp.concatenate([ratio] * plan.blocks, 0) * first_values[...]
+    kept = weighted(values)
+    step_len = norm_next / (ridge + inner(values, kept.astype(jnp.float32)))
+    gather_start(2, kept, [step_len, ratio])
+    step_col, ratio_col = gather_finish(2)
+    transposed()
+    for at in range(plan.width // LANES):
+        cols = slice(at * LANES, (at + 1) * LANES)
+        along = scal[:, cols] + ratio_col * direc[:, cols]
+        ahead = solut[:, cols] + step_col * along
+        left = resid[:, cols] - step_col * (image[:, cols] + ridge_row[:, cols] * along)
+        solution_out[cols, :] = ahead.T
+        residual_out[cols, :] = left.T
+
+    for bits in range(1, slabs):
+        show_copy(bits).wait_send()
+        for part in range(2):
+            block_copy(bits, part).wait_send()
+    for phase in range(3):
+        here = gathered.at[phase, core, chip]
+        for step in range(1, chips):
+            to = other(step)
+            remote(here, here, gather_send.at[phase, to], gather_recv.at[phase, chip], device(to)).wait_send()
+        mine = gathered.at[phase, core]
+        remote(mine, mine, relay_send.at[phase], relay_recv.at[phase], partner).wait_send()
+    for turn in range(2):
+        remote(sums.at[turn, 1 - core], received.at[turn], pair_send.at[turn], pair_recv.at[turn], partner).wait_send()
+        for step in range(1, chips):
+            to = other(step)
+            remote(sent.at[turn, to], folded_in.at[turn, chip], fold_send.at[turn, to], fold_recv.at[turn, chip], device(to)).wait_send()
+        mine = whole.at[turn, core]
+        remote(mine, mine, whole_send.at[turn], whole_recv.at[turn], partner).wait_send()
+
+
+def fused_shards(design, observed, slab_counts, gap_mask, filter_taps, kaula_diag, precond):
+    epoch_rows, coef_rows = design.shape
+    columns = observed.shape[1]
+    slabs, coefs = lax.axis_size("tm"), lax.axis_size("coef")
+    plan = Plan(slabs, coefs, epoch_rows, coef_rows, columns)
+    wide, chips, group = plan.width, plan.chips, plan.group
+    f32, bf16 = jnp.float32, jnp.bfloat16
+    vmem = pl.BlockSpec(memory_space=pltpu.VMEM)
+    sem = pltpu.SemaphoreType.DMA
+    shape = jax.ShapeDtypeStruct((wide, columns), f32)
+    outs = pl.pallas_call(
+        functools.partial(fused, plan),
+        out_shape=(shape, shape),
+        in_specs=[pl.BlockSpec(memory_space=pl.ANY), vmem, vmem, pl.BlockSpec(memory_space=pltpu.SMEM), vmem, vmem, vmem],
+        out_specs=(vmem, vmem),
+        scratch_shapes=[
+            pltpu.VMEM((slabs, epoch_rows, wide), bf16),
+            pltpu.VMEM((chips, 2 * group, epoch_rows), f32),
+            pltpu.VMEM((slabs, 2 * group, epoch_rows), f32),
+            pltpu.VMEM((2, 2, slabs // 2 + 1, columns, epoch_rows), f32),
+            pltpu.VMEM((2, chips, group, plan.message), bf16),
+            pltpu.VMEM((2, slabs // 2 + 1, columns, epoch_rows), f32),
+            pltpu.VMEM((chips, group, plan.message), f32),
+            pltpu.VMEM((2, 2, group, plan.message), f32),
+            pltpu.VMEM((2, group, plan.message), f32),
+            pltpu.VMEM((slabs, columns, epoch_rows), bf16),
+            pltpu.VMEM((3, 2, chips, group, plan.message), bf16),
+            pltpu.VMEM((2, chips, group, plan.message), bf16),
+            pltpu.VMEM((columns, wide), f32),
+            pltpu.VMEM((columns, wide), f32),
+            pltpu.VMEM((columns, wide), f32),
+            pltpu.VMEM((columns, wide), f32),
+            pltpu.VMEM((columns, wide), f32),
+            pltpu.VMEM((plan.blocks * group, LANES), f32),
+            sem(()), sem((2, slabs)), sem((2, slabs)), sem((slabs,)), sem((slabs,)), sem((2,)), sem((2,)),
+            sem((2, chips)), sem((2, chips)), sem((2,)), sem((2,)),
+            sem((3, chips)), sem((3, chips)), sem((3,)), sem((3,)),
+        ],
+        compiler_params=pltpu.CompilerParams(
+            collective_id=0, has_side_effects=True, vmem_limit_bytes=48 * 1024 * 1024
+        ),
+    )(design, observed, gap_mask[None], slab_counts, filter_taps[None], kaula_diag[None], precond[None])
+    start = lax.axis_index("tm") * plan.owned
+    low = start - plan.first_tile(lax.axis_index("tm")) * LANES
+    return tuple(lax.dynamic_slice_in_dim(out, low, plan.owned, 0) for out in outs)
+
+
+def shards(*arrays):
+    design, observed, filter_taps = arrays[0], arrays[1], arrays[4]
+    sizes = (lax.axis_size("tm"), lax.axis_size("coef"), *design.shape, observed.shape[1], filter_taps.shape[0])
+    return fused_shards(*arrays) if fits(*sizes) else general_shards(*arrays)
+
+
 def solution(mesh):
     placed = (P("tm", "coef"), P("tm", None), P("tm"), P("tm"), P(), P("coef"), P("coef"))
     return jax.shard_map(

time: 510 us -> 232 us (0.45)
  waiting for transfers between devices: 409 us -> 0 us
  Pallas kernels: 0 us -> 225 us
  matrix products: 33.9 us -> 0 us
  local copies, waits for them, and re-layouts: 31.5 us -> 5.19 us
  between operations: 14.8 us -> 1.31 us
  other arithmetic: 11.1 us -> 0 us
  starting transfers between devices: 7.75 us -> 0 us
    psum x2 -> x0, waiting for transfers between devices: 259 us -> none  [summed(): total = lax.psum(jnp.concatenate([partial] + rows, 0), ('tm', 'coef'))]
    pallas_call x0 -> x1, Pallas kernels: none -> 225 us  [fused_shards(): pl.pallas_call(functools.partial(fused, plan), out_shape=(shape, shape),...]
    all_gather x1 -> x0, waiting for transfers between devices: 150 us -> none  [shards(): gathered = lax.all_gather(packed, 'tm', axis=0, tiled=False)]
    dot_general x17 -> x0, matrix products: 33.9 us -> none  [the longest x3 12.8 us: transposed(): lax.dot_general(block, filtered, (((0,), (0,)), ((), ())), preferred_elem...]
    unnamed x41 -> x6, local copies, waits for them, and re-layouts: 10.8 us -> 2.23 us
    all_to_all x1 -> x0, starting transfers between devices: 7.45 us -> none  [shards(): lax.all_to_all(design, 'tm', split_axis=1, concat_axis=0, tiled=True)]
    slice x9 -> x0, local copies, waits for them, and re-layouts: 5.51 us -> none  [the longest x6 3.38 us: forward(): previous = jnp.concatenate([jnp.zeros_like(blocks[:1]), blocks[:-1]], 0)]
  transfers between devices with their start and end apart: 4 -> 0, of which waited for: 3 -> 0; matrix products, arithmetic and copies ran while one was open for 2% -> 0% of each run, Pallas kernels for 0% -> 0%
where the time goes in v1:
time: 232 us
  Pallas kernels  225 us (97%)
  local copies, waits for them, and re-layouts  5.19 us (2%)
    pallas_call x1, Pallas kernels, fused_shards(): pl.pallas_call(functools.partial(fused, plan), out_shape=(shape, shape),...  225 us

profile of v1, /device:TPU:0, one launch (start us, length us, event | category | flops | bytes accessed | tf_op | source)
XLA Modules:
  0.0 231.6 jit_solution(11768128333416045070)
XLA Ops:
  1.3 0.8 broadcast_in_dim.14.kaula
  2.1 0.8 broadcast_in_dim.15.precond
  3.0 0.0 copy-start
  3.0 0.9 copy-done
  3.9 0.0 copy-start.1
  3.9 0.7 copy-done.1
  4.6 0.0 copy-start.2
  4.6 0.7 copy-done.2
  5.2 225.1 %shard_map.86 = (f32[1664,128]{1,0:T(8,128)S(1)}, f32[1664,128]{1,0:T(8,128)S(1)}) custom-call(bf16[256,12544]{1,0:T(8,128)(2,1)} %design.1, f32[256,128]{1,0:T(8,128)S(1)} %copy-done, s32[1,256]{1,0:T(1,128)S(1)} %bitcast.2, s32[1]{0:T(128)S(6)} %copy.9.counts, f32[1,128]{1,0:T(1,128)S(1)} %bitcast.3, f32[1,12544]{1,0:T(1,128)S(1)} %broadcast_in_dim.14.kaula, ...), custom_call_target="tpu_custom_call" | custom-call | tf_op jit(solution)/shard_map/pallas_call | solution.py:455
  230.3 1.3 constant_dynamic-slice_fusion
Async XLA Ops:
  3.0 0.9 copy-start
  3.9 0.7 copy-start.1
  4.6 0.7 copy-start.2

commit v2 on v0

--- a/solution.py
+++ b/solution.py
@@ -1,6 +1,10 @@
+import functools
+
 import jax
 import jax.numpy as jnp
 from jax import lax
+from jax.experimental import pallas as pl
+from jax.experimental.pallas import tpu as pltpu
 from jax.sharding import PartitionSpec as P
 
 ITERS = 2
@@ -39,7 +43,7 @@
     return result.reshape(values.shape)
 
 
-def shards(design, observed, slab_counts, gap_mask, filter_taps, kaula_diag, precond):
+def general_shards(design, observed, slab_counts, gap_mask, filter_taps, kaula_diag, precond):
     epoch_rows, coef_rows = design.shape
     columns = observed.shape[1]
     slabs = lax.axis_size("tm")
@@ -99,6 +103,591 @@
     return (solution, residual)
 
 
+LANES = 128
+GROUP = 8
+MESH = pl.DeviceIdType.MESH
+NN = ((1,), (0,))
+NT = ((1,), (1,))
+
+
+class Plan:
+    def __init__(self, slabs, coefs, epoch_rows, coef_rows, columns):
+        self.slabs, self.coefs, self.epoch_rows, self.columns = slabs, coefs, epoch_rows, columns
+        self.tiles = coef_rows // LANES
+        self.owned = coef_rows // slabs
+        self.full = self.owned // LANES - 1
+        self.rest = self.owned % LANES
+        self.packed_rows = epoch_rows * self.rest // LANES
+        self.mixed_at = self.full * LANES
+        self.width = (self.full + 2) * LANES
+        self.cut = self.full * 3 // 4 * LANES
+        self.across = coefs // 2
+        self.chips = slabs * self.across
+        self.blocks = slabs * epoch_rows // LANES
+        self.half = slabs * epoch_rows // 2
+        self.message = self.half + LANES
+
+    def first_tile(self, owner):
+        return lax.div(owner * self.owned, LANES)
+
+
+def fits(slabs, coefs, epoch_rows, coef_rows, columns, taps):
+    if slabs & (slabs - 1) or slabs < 4 or coefs % 2 or epoch_rows % (2 * LANES) or coef_rows % LANES:
+        return False
+    if coef_rows % slabs or taps != LANES or columns != LANES or columns != GROUP * slabs * coefs // 2:
+        return False
+    owned = coef_rows // slabs
+    rest = owned % LANES
+    return owned >= 4 * LANES and rest >= 16 and LANES % rest == 0
+
+
+def flipped(index, bits, count):
+    result, weight = 0, 1
+    while weight < count:
+        bit = lax.rem(lax.div(index, weight), 2)
+        result = result + weight * (1 - bit if bits & weight else bit)
+        weight *= 2
+    return result
+
+
+def pieces(values):
+    high = values.astype(jnp.bfloat16).astype(jnp.float32)
+    left = values - high
+    middle = left.astype(jnp.bfloat16).astype(jnp.float32)
+    low = (left - middle).astype(jnp.bfloat16).astype(jnp.float32)
+    return high + pltpu.roll(middle, 8, 1) + pltpu.roll(low, 16, 1)
+
+
+def joined(values, at):
+    lane = lax.broadcasted_iota(jnp.int32, values.shape, 1)
+    taken = (lane % 8 == at) & (lane < 24)
+    return jnp.sum(jnp.where(taken, values, 0.0), 1, keepdims=True)
+
+
+def in_lanes(terms, rows):
+    lane = lax.broadcasted_iota(jnp.int32, (rows, LANES), 1)
+    result = jnp.zeros((rows, LANES), jnp.float32)
+    for at, term in enumerate(terms):
+        result = jnp.where(lane == at, term, result)
+    return result
+
+
+def product(left, right, contract, precision=None):
+    return lax.dot_general(
+        left, right, (contract, ((), ())), precision=precision, preferred_element_type=jnp.float32
+    )
+
+
+def fused(plan, design, observed_in, gap_in, counts, taps_in, kaula_in, precond_in, solution_out, residual_out,
+          observed, gap, taps, kaula, precond,
+          block, edges, packed, loose, shown, seen, early, sums, received, total, sent, folded_in, sent_terms, terms_in,
+          whole, folded, filtered, gathered, resid, direc, scal, solut, first_values,
+          own_sem, small_sem, edge_sem, block_send, block_recv, show_send, show_recv, early_send, early_recv,
+          early_relay_send, early_relay_recv, pair_send, pair_recv, fold_send, fold_recv, term_send, term_recv,
+          whole_send, whole_recv, gather_send, gather_recv, relay_send, relay_recv):
+    slabs, chips, rows = plan.slabs, plan.chips, plan.epoch_rows
+    half_slabs, half_chips, half_blocks = slabs // 2, chips // 2, plan.blocks // 2
+    slab, coef = lax.axis_index("tm"), lax.axis_index("coef")
+    across, core = lax.div(coef, 2), lax.rem(coef, 2)
+    chip = slab * plan.across + across
+    near_chip = lax.rem(chip, half_chips)
+    this_half = lax.div(chip, half_chips)
+    partner = {"tm": slab, "coef": 2 * across + 1 - core}
+
+    def device(at):
+        return {"tm": lax.div(at, plan.across), "coef": 2 * lax.rem(at, plan.across) + core}
+
+    def other(step):
+        return lax.rem(chip + step, chips)
+
+    def near_other(step):
+        return lax.rem(near_chip + step, half_chips)
+
+    def remote(src, dst, send, recv, target):
+        return pltpu.make_async_remote_copy(
+            src_ref=src, dst_ref=dst, send_sem=send, recv_sem=recv, device_id=target, device_id_type=MESH
+        )
+
+    barrier = pltpu.get_barrier_semaphore()
+    for step in range(1, chips):
+        pl.semaphore_signal(barrier, inc=1, device_id=device(other(step)), device_id_type=MESH)
+    pl.semaphore_signal(barrier, inc=1, device_id=partner, device_id_type=MESH)
+
+    small = [
+        pltpu.make_async_copy(src, dst, small_sem.at[at])
+        for at, (src, dst) in enumerate(
+            ((observed_in, observed), (gap_in, gap), (taps_in, taps), (kaula_in, kaula), (precond_in, precond))
+        )
+    ]
+    for copy in small:
+        copy.start()
+    first = plan.first_tile(slab)
+    offset = slab * plan.owned - first * LANES
+
+    def tile_columns(tile, size):
+        return pl.ds(pl.multiple_of(tile * LANES, LANES), size)
+
+    own = pltpu.make_async_copy(
+        design.at[:, tile_columns(first + 1, plan.mixed_at)], block.at[slab, :, pl.ds(0, plan.mixed_at)], own_sem
+    )
+    own.start()
+    edge_copies = []
+    for owner in range(slabs):
+        begin = owner * plan.owned // LANES
+        for at, tile in enumerate((begin, begin + plan.full + 1)):
+            edge_copies.append(pltpu.make_async_copy(
+                design.at[:, pl.ds(tile * LANES, LANES)], edges.at[owner, at], edge_sem.at[owner, at]
+            ))
+            edge_copies[-1].start()
+
+    for copy in small[:3]:
+        copy.wait()
+    place = lax.broadcasted_iota(jnp.int32, (1, rows), 1)
+    present = jnp.concatenate([gap[at:at + 1, :] for at in range(rows // LANES)], 1)
+    weight_row = jnp.where((present == 1) & (place < counts[0]), 1.0, 0.0)
+    turned = observed[...].T * weight_row
+    shown[:, :GROUP, :] = turned.reshape(chips, GROUP, rows)
+    shown[:, GROUP:, :] = jnp.broadcast_to(weight_row[None], (chips, GROUP, rows))
+    seen[slab] = shown[2 * near_chip + core]
+
+    def block_copy(bits, part):
+        peer = flipped(slab, bits, slabs)
+        tile = plan.first_tile(peer) + 1
+        if part == 0:
+            src, dst = design.at[:, tile_columns(tile, plan.cut)], block.at[slab, :, pl.ds(0, plan.cut)]
+        elif part == 1:
+            src = design.at[:, tile_columns(tile + plan.cut // LANES, plan.mixed_at - plan.cut)]
+            dst = block.at[slab, :, pl.ds(plan.cut, plan.mixed_at - plan.cut)]
+        elif part == 2:
+            src, dst = packed.at[peer, pl.ds(0, rows)], block.at[slab, :, pl.ds(plan.mixed_at, LANES)]
+        else:
+            src, dst = packed.at[peer, pl.ds(rows, plan.packed_rows)], loose.at[slab]
+        return remote(src, dst, block_send.at[part, peer], block_recv.at[part, slab], {"tm": peer, "coef": coef})
+
+    def block_arrival(bits, part):
+        peer = flipped(slab, bits, slabs)
+        if part == 0:
+            dst = block.at[peer, :, pl.ds(0, plan.cut)]
+        elif part == 1:
+            dst = block.at[peer, :, pl.ds(plan.cut, plan.mixed_at - plan.cut)]
+        elif part == 2:
+            dst = block.at[peer, :, pl.ds(plan.mixed_at, LANES)]
+        else:
+            dst = loose.at[peer]
+        return remote(dst, dst, block_send.at[part, peer], block_recv.at[part, peer], {"tm": peer, "coef": coef})
+
+    def show_copy(bits):
+        peer = flipped(slab, bits, slabs)
+        src = shown.at[2 * lax.rem(peer * plan.across + across, half_chips) + core]
+        return remote(src, seen.at[slab], show_send.at[peer], show_recv.at[slab], {"tm": peer, "coef": coef})
+
+    def show_arrival(bits):
+        peer = flipped(slab, bits, slabs)
+        return remote(seen.at[peer], seen.at[peer], show_send.at[peer], show_recv.at[peer], {"tm": peer, "coef": coef})
+
+    pl.semaphore_wait(barrier, chips)
+    for bits in range(1, slabs):
+        show_copy(bits).start()
+    for bits in range(1, half_slabs):
+        block_copy(bits, 0).start()
+        block_copy(bits, 1).start()
+    for bits in range(half_slabs, slabs):
+        block_copy(bits, 0).start()
+
+    for copy in edge_copies:
+        copy.wait()
+    lane_row = lax.broadcasted_iota(jnp.int32, (1, LANES), 1)
+    for owner in range(slabs):
+        skip = owner * plan.owned % LANES
+        ahead = edges[owner, 0].astype(jnp.float32)
+        behind = edges[owner, 1].astype(jnp.float32)
+        packed[owner, :rows] = jnp.where(lane_row >= skip, ahead, behind).astype(jnp.bfloat16)
+        tight = jnp.zeros((plan.packed_rows, LANES), jnp.float32)
+        for at in range(LANES // plan.rest):
+            part = behind[at * plan.packed_rows:(at + 1) * plan.packed_rows]
+            shift = (at * plan.rest - skip) % LANES
+            part = pltpu.roll(part, shift, 1) if shift else part
+            tight = jnp.where(lax.div(lane_row, plan.rest) == at, part, tight)
+        packed[owner, rows:] = tight.astype(jnp.bfloat16)
+    for bits in range(1, slabs):
+        block_copy(bits, 2).start()
+        block_copy(bits, 3).start()
+
+    def unpack(at):
+        tight = loose[at].astype(jnp.float32)
+        for piece in range(LANES // plan.rest):
+            part = pltpu.roll(tight, LANES - piece * plan.rest, 1) if piece else tight
+            part = jnp.where(lane_row < plan.rest, part, 0.0).astype(jnp.bfloat16)
+            block[at, piece * plan.packed_rows:(piece + 1) * plan.packed_rows, plan.mixed_at + LANES:] = part
+
+    block[slab, :, plan.mixed_at:plan.mixed_at + LANES] = packed[slab, :rows]
+    loose[slab] = packed[slab, rows:]
+    unpack(slab)
+
+    base = jnp.concatenate([taps[...], jnp.zeros((1, LANES), jnp.float32)], 1)
+    shifted = pltpu.roll(jnp.broadcast_to(base, (LANES, 2 * LANES)), 0, 1, stride=1, stride_axis=0)
+    lower, upper = shifted[:, :LANES], shifted[:, LANES:]
+    blank = jnp.zeros((GROUP, LANES), jnp.float32)
+
+    for bits in range(1, slabs):
+        show_arrival(bits).wait_recv()
+
+    def stack(ref, low):
+        return jnp.concatenate(
+            [ref[at, low:low + GROUP, j * LANES:(j + 1) * LANES] for at in range(slabs) for j in range(rows // LANES)], 0
+        )
+
+    weight = stack(seen, GROUP)
+
+    def weighted(values):
+        entering = weight * values
+        before = jnp.concatenate([blank, entering[:-GROUP]], 0)
+        inner = product(entering, lower, NN, lax.Precision.HIGHEST) + product(before, upper, NN, lax.Precision.HIGHEST)
+        after = jnp.concatenate([inner[GROUP:], blank], 0)
+        outer = product(inner, lower, NT, lax.Precision.HIGHEST) + product(after, upper, NT, lax.Precision.HIGHEST)
+        return (weight * outer).astype(jnp.bfloat16)
+
+    kept = weighted(stack(seen, 0)).astype(jnp.float32)
+    for j in range(plan.blocks):
+        early[core, near_chip, :, j * LANES:(j + 1) * LANES] = kept[j * GROUP:(j + 1) * GROUP].astype(jnp.bfloat16)
+    for step in range(1, half_chips):
+        to = near_other(step)
+        here = early.at[core, near_chip]
+        target = device(this_half * half_chips + to)
+        remote(here, here, early_send.at[to], early_recv.at[near_chip], target).start()
+    for bits in range(half_slabs, slabs):
+        block_copy(bits, 1).start()
+
+    small[3].wait()
+    small[4].wait()
+
+    def local_row(table):
+        inside = [table[pl.ds(first + 1 + at, 1), :] for at in range(plan.full)]
+        ahead, behind = table[pl.ds(first, 1), :], table[pl.ds(first + plan.full + 1, 1), :]
+        moved = pltpu.roll(jnp.broadcast_to(behind, (GROUP, LANES)), lax.rem(LANES - offset, LANES), 1)[:1]
+        mixed = jnp.where(lane_row >= offset, ahead, behind)
+        return jnp.concatenate(inside + [mixed, jnp.where(lane_row < plan.rest, moved, 0.0)], 1)
+
+    ridge_row, scale_row = local_row(kaula), local_row(precond)
+
+    def early_arrival(step):
+        at = near_other(step)
+        here = early.at[core, at]
+        return remote(here, here, early_send.at[at], early_recv.at[at], device(this_half * half_chips + at))
+
+    for step in range(1, half_chips):
+        early_arrival(step).wait_recv()
+    mine, theirs = early.at[core], early.at[1 - core]
+    remote(mine, mine, early_relay_send, early_relay_recv, partner).start()
+    remote(theirs, theirs, early_relay_send, early_relay_recv, partner).wait_recv()
+    for at in range(slabs):
+        span = slice(at * rows, (at + 1) * rows)
+        both = jnp.stack([early[0, :, :, span].astype(jnp.float32), early[1, :, :, span].astype(jnp.float32)], 1)
+        filtered[:, span] = both.reshape(plan.columns, rows).astype(jnp.bfloat16)
+
+    def series(at):
+        return filtered[:, pl.ds(pl.multiple_of(at * rows, rows), rows)]
+
+    def over(terms):
+        return jnp.sum(terms, 1, keepdims=True)
+
+    own.wait()
+    spans = (slice(0, plan.cut), slice(plan.cut, plan.width))
+    for part, span in enumerate(spans):
+        resid[:, span] = product(series(slab), block[slab, :, span], NN)
+        for bits in range(1, slabs):
+            peer = flipped(slab, bits, slabs)
+            for piece in ((0,), (1, 2, 3))[part]:
+                block_arrival(bits, piece).wait_recv()
+            if part:
+                unpack(peer)
+            resid[:, span] += product(series(peer), block[peer, :, span], NN)
+        direc[:, span] = scale_row[:, span] * resid[:, span]
+        if part == 0:
+            low = direc[:, span].astype(jnp.bfloat16)
+
+            def body(at, carry):
+                sums[0, at] = product(low, block[at, :, :plan.cut], NT)
+                return carry
+
+            lax.fori_loop(0, slabs, body, 0)
+
+    def pair_copy(turn, j):
+        src = sums.at[turn, (1 - core) * half_slabs + j]
+        return remote(src, received.at[turn, j], pair_send.at[turn, j], pair_recv.at[turn, j], partner)
+
+    def fold_copy(turn, j, step):
+        to = other(step)
+        src, dst = sent.at[turn, j, to], folded_in.at[turn, j, chip]
+        return remote(src, dst, fold_send.at[turn, j, to], fold_recv.at[turn, j, chip], device(to))
+
+    def fold_arrival(turn, j, at):
+        here = folded_in.at[turn, j, at]
+        return remote(here, here, fold_send.at[turn, j, at], fold_recv.at[turn, j, at], device(at))
+
+    def term_copy(turn, step):
+        to = other(step)
+        src, dst = sent_terms.at[turn, to], terms_in.at[turn, chip]
+        return remote(src, dst, term_send.at[turn, to], term_recv.at[turn, chip], device(to))
+
+    def term_arrival(turn, at):
+        here = terms_in.at[turn, at]
+        return remote(here, here, term_send.at[turn, at], term_recv.at[turn, at], device(at))
+
+    def each_chip(action):
+        def body(step, carry):
+            action(step)
+            return carry
+
+        lax.fori_loop(1, chips, body, 0)
+
+    def summed(turn, low, terms, span):
+        scalars = in_lanes(terms, plan.columns)
+        sent_terms[turn] = pieces(scalars).reshape(chips, GROUP, LANES).astype(jnp.bfloat16)
+        terms_in[turn, chip] = sent_terms[turn, chip]
+        each_chip(lambda step: term_copy(turn, step).start())
+
+        def partial(at):
+            value = product(low, block[at, :, span], NT)
+            return value + sums[turn, at] if turn == 0 else value
+
+        def give(j, carry):
+            at = (1 - core) * half_slabs + j
+            sums[turn, at] = partial(at)
+            pair_copy(turn, j).start()
+            return carry
+
+        lax.fori_loop(0, half_slabs, give, 0)
+
+        def keep(j, carry):
+            value = partial(core * half_slabs + j)
+            pair_copy(turn, j).wait_recv()
+            value = (value + received[turn, j]).reshape(chips, GROUP, rows)
+            total[j] = value
+            sent[turn, j] = value.astype(jnp.bfloat16)
+            each_chip(lambda step: fold_copy(turn, j, step).start())
+            return carry
+
+        lax.fori_loop(0, half_slabs, keep, 0)
+
+        def take(step, carry):
+            at = other(step)
+            term_arrival(turn, at).wait_recv()
+            return carry + terms_in[turn, at].astype(jnp.float32)
+
+        whole[turn, core, :, plan.half:] = lax.fori_loop(1, chips, take, terms_in[turn, chip].astype(jnp.float32))
+        for j in range(half_slabs):
+            def arrive(step, carry):
+                at = other(step)
+                fold_arrival(turn, j, at).wait_recv()
+                return carry + folded_in[turn, j, at].astype(jnp.float32)
+
+            whole[turn, core, :, j * rows:(j + 1) * rows] = lax.fori_loop(1, chips, arrive, total[j, chip])
+        mine, theirs = whole.at[turn, core], whole.at[turn, 1 - core]
+        remote(mine, mine, whole_send.at[turn], whole_recv.at[turn], partner).start()
+        remote(theirs, theirs, whole_send.at[turn], whole_recv.at[turn], partner).wait_recv()
+        values = jnp.concatenate(
+            [whole[turn, half, :, j * LANES:(j + 1) * LANES] for half in range(2) for j in range(half_blocks)], 0
+        )
+        scalars = whole[turn, 0, :, plan.half:] + whole[turn, 1, :, plan.half:]
+        return values, [joined(scalars, at) for at in range(len(terms))]
+
+    def gather_copy(phase, step):
+        to = other(step)
+        here = gathered.at[phase, core, chip]
+        return remote(here, here, gather_send.at[phase, to], gather_recv.at[phase, chip], device(to))
+
+    def gather_arrival(phase, at):
+        here = gathered.at[phase, core, at]
+        return remote(here, here, gather_send.at[phase, at], gather_recv.at[phase, at], device(at))
+
+    def relay_copy(phase, at):
+        here = gathered.at[phase, core, at]
+        return remote(here, here, relay_send.at[phase, at], relay_recv.at[phase, at], partner)
+
+    def relay_arrival(phase, at):
+        here = gathered.at[phase, 1 - core, at]
+        return remote(here, here, relay_send.at[phase, at], relay_recv.at[phase, at], partner)
+
+    def shared(phase, values, terms):
+        wide = values.astype(jnp.float32)
+        for half in range(2):
+            for j in range(half_blocks):
+                low = (half * half_blocks + j) * GROUP
+                folded[half, :, j * LANES:(j + 1) * LANES] = wide[low:low + GROUP]
+            folded[half, :, plan.half:] = pieces(in_lanes(terms, GROUP))
+        gathered[phase, core, chip] = folded[core].astype(jnp.bfloat16)
+        each_chip(lambda step: gather_copy(phase, step).start())
+        relay_copy(phase, chip).start()
+
+        def pass_on(step):
+            at = other(step)
+            gather_arrival(phase, at).wait_recv()
+            relay_copy(phase, at).start()
+
+        each_chip(pass_on)
+        relay_arrival(phase, chip).wait_recv()
+        each_chip(lambda step: relay_arrival(phase, other(step)).wait_recv())
+        for half in range(2):
+            for j in range(half_slabs):
+                part = gathered[phase, half, :, :, j * rows:(j + 1) * rows].astype(jnp.float32)
+                low = half * plan.half + j * rows
+                filtered[:, low:low + rows] = part.reshape(plan.columns, rows).astype(jnp.bfloat16)
+        scalars = gathered[phase, 0, :, :, plan.half:].astype(jnp.float32).reshape(plan.columns, LANES)
+        return [joined(scalars, at) for at in range(len(terms))]
+
+    def inner(left, right):
+        together = (left * right).reshape(plan.blocks, GROUP, LANES)
+        return over(jnp.sum(together, 0))
+
+    chunks = [slice(low, min(low + 2 * LANES, plan.width)) for low in range(0, plan.width, 2 * LANES)]
+
+    def transposed(span):
+        part = block[:, :, span]
+        return product(filtered[...], part.reshape(slabs * rows, part.shape[2]), NN)
+
+    ridged = ridge_row * direc[...]
+    terms = [over(resid[...] * direc[...]), over(ridged * direc[...])]
+    values, (norm, ridge) = summed(0, direc[:, spans[1]].astype(jnp.bfloat16), terms, spans[1])
+    first_values[...] = values
+    kept = weighted(values)
+    step_len = norm / (ridge + inner(values, kept.astype(jnp.float32)))
+    (step_col,) = shared(0, kept, [step_len])
+    terms = [0.0, 0.0, 0.0]
+    for span in chunks:
+        along, ridge_part = direc[:, span], ridge_row[:, span]
+        left = resid[:, span] - step_col * (transposed(span) + ridge_part * along)
+        ahead = scale_row[:, span] * left
+        resid[:, span] = left
+        solut[:, span] = step_col * along
+        scal[:, span] = ahead
+        ridged = ridge_part * ahead
+        added = (over(left * ahead), over(ridged * ahead), over(ridged * along))
+        terms = [term + more for term, more in zip(terms, added)]
+    fresh, (norm_next, own_ridge, cross) = summed(1, scal[...].astype(jnp.bfloat16), terms, slice(0, plan.width))
+    ratio = norm_next / norm
+    ridge = own_ridge + ratio * (2.0 * cross + ratio * ridge)
+    values = fresh + jnp.concatenate([ratio] * plan.blocks, 0) * first_values[...]
+    kept = weighted(values)
+    step_len = norm_next / (ridge + inner(values, kept.astype(jnp.float32)))
+    step_col, ratio_col = shared(1, kept, [step_len, ratio])
+
+    def put(out, tile, value):
+        out[pl.ds(pl.multiple_of((tile + 2) * LANES - offset, plan.rest), LANES), :] = value
+
+    held = {}
+    for span in chunks:
+        along = scal[:, span] + ratio_col * direc[:, span]
+        ahead = solut[:, span] + step_col * along
+        left = resid[:, span] - step_col * (transposed(span) + ridge_row[:, span] * along)
+        for low in range(0, span.stop - span.start, LANES):
+            held[(span.start + low) // LANES] = (ahead[:, low:low + LANES].T, left[:, low:low + LANES].T)
+        for tile in [tile for tile in held if tile < plan.full]:
+            new_ahead, new_left = held.pop(tile)
+            put(solution_out, tile, new_ahead)
+            put(residual_out, tile, new_left)
+    mixed = held[plan.full]
+    last = held[plan.full + 1]
+    for out, first_value, second in ((solution_out, mixed[0], last[0]), (residual_out, mixed[1], last[1])):
+        low = pl.multiple_of(LANES - offset, plan.rest)
+        out[pl.ds(low, LANES), :] = first_value
+        low = pl.multiple_of((plan.full + 2) * LANES - offset, plan.rest)
+        out[pl.ds(low, LANES), :] = first_value
+        low = (plan.full + 2) * LANES
+        out[low:low + plan.rest, :] = second[:plan.rest]
+
+    for bits in range(1, slabs):
+        show_copy(bits).wait_send()
+        for part in range(4):
+            block_copy(bits, part).wait_send()
+    for step in range(1, half_chips):
+        to = near_other(step)
+        here = early.at[core, near_chip]
+        target = device(this_half * half_chips + to)
+        remote(here, here, early_send.at[to], early_recv.at[near_chip], target).wait_send()
+    mine = early.at[core]
+    remote(mine, mine, early_relay_send, early_relay_recv, partner).wait_send()
+    for turn in range(2):
+        for j in range(half_slabs):
+            pair_copy(turn, j).wait_send()
+            each_chip(lambda step: fold_copy(turn, j, step).wait_send())
+        each_chip(lambda step: term_copy(turn, step).wait_send())
+        mine = whole.at[turn, core]
+        remote(mine, mine, whole_send.at[turn], whole_recv.at[turn], partner).wait_send()
+        each_chip(lambda step: gather_copy(turn, step).wait_send())
+        relay_copy(turn, chip).wait_send()
+        each_chip(lambda step: relay_copy(turn, other(step)).wait_send())
+
+
+def fused_shards(design, observed, slab_counts, gap_mask, filter_taps, kaula_diag, precond):
+    epoch_rows, coef_rows = design.shape
+    columns = observed.shape[1]
+    slabs, coefs = lax.axis_size("tm"), lax.axis_size("coef")
+    plan = Plan(slabs, coefs, epoch_rows, coef_rows, columns)
+    wide, chips, message = plan.width, plan.chips, plan.message
+    half_slabs, half_chips = slabs // 2, chips // 2
+    f32, bf16 = jnp.float32, jnp.bfloat16
+    vmem = pl.BlockSpec(memory_space=pltpu.VMEM)
+    hbm = pl.BlockSpec(memory_space=pltpu.HBM)
+    sem = pltpu.SemaphoreType.DMA
+    shape = jax.ShapeDtypeStruct((wide + LANES, columns), f32)
+    tiles = (plan.tiles, LANES)
+    outs = pl.pallas_call(
+        functools.partial(fused, plan),
+        out_shape=(shape, shape),
+        in_specs=[hbm, hbm, hbm, pl.BlockSpec(memory_space=pltpu.SMEM), hbm, hbm, hbm],
+        out_specs=(vmem, vmem),
+        scratch_shapes=[
+            pltpu.VMEM((epoch_rows, columns), f32),
+            pltpu.VMEM((epoch_rows // LANES, LANES), jnp.int32),
+            pltpu.VMEM((1, LANES), f32),
+            pltpu.VMEM(tiles, f32),
+            pltpu.VMEM(tiles, f32),
+            pltpu.VMEM((slabs, epoch_rows, wide), bf16),
+            pltpu.VMEM((slabs, 2, epoch_rows, LANES), bf16),
+            pltpu.VMEM((slabs, epoch_rows + plan.packed_rows, LANES), bf16),
+            pltpu.VMEM((slabs, plan.packed_rows, LANES), bf16),
+            pltpu.VMEM((chips, 2 * GROUP, epoch_rows), f32),
+            pltpu.VMEM((slabs, 2 * GROUP, epoch_rows), f32),
+            pltpu.VMEM((2, half_chips, GROUP, slabs * epoch_rows), bf16),
+            pltpu.VMEM((2, slabs, columns, epoch_rows), f32),
+            pltpu.VMEM((2, half_slabs, columns, epoch_rows), f32),
+            pltpu.VMEM((half_slabs, chips, GROUP, epoch_rows), f32),
+            pltpu.VMEM((2, half_slabs, chips, GROUP, epoch_rows), bf16),
+            pltpu.VMEM((2, half_slabs, chips, GROUP, epoch_rows), bf16),
+            pltpu.VMEM((2, chips, GROUP, LANES), bf16),
+            pltpu.VMEM((2, chips, GROUP, LANES), bf16),
+            pltpu.VMEM((2, 2, GROUP, message), f32),
+            pltpu.VMEM((2, GROUP, message), f32),
+            pltpu.VMEM((columns, slabs * epoch_rows), bf16),
+            pltpu.VMEM((2, 2, chips, GROUP, message), bf16),
+            pltpu.VMEM((columns, wide), f32),
+            pltpu.VMEM((columns, wide), f32),
+            pltpu.VMEM((columns, wide), f32),
+            pltpu.VMEM((columns, wide), f32),
+            pltpu.VMEM((plan.blocks * GROUP, LANES), f32),
+            sem(()), sem((5,)), sem((slabs, 2)), sem((4, slabs)), sem((4, slabs)), sem((slabs,)), sem((slabs,)),
+            sem((half_chips,)), sem((half_chips,)), sem(()), sem(()),
+            sem((2, half_slabs)), sem((2, half_slabs)), sem((2, half_slabs, chips)), sem((2, half_slabs, chips)),
+            sem((2, chips)), sem((2, chips)), sem((2,)), sem((2,)),
+            sem((2, chips)), sem((2, chips)), sem((2, chips)), sem((2, chips)),
+        ],
+        compiler_params=pltpu.CompilerParams(
+            collective_id=0, has_side_effects=True, vmem_limit_bytes=48 * 1024 * 1024
+        ),
+    )(
+        design, observed, gap_mask.reshape(-1, LANES), slab_counts, filter_taps[None],
+        kaula_diag.reshape(tiles), precond.reshape(tiles),
+    )
+    return tuple(out[LANES:LANES + plan.owned] for out in outs)
+
+
+def shards(*arrays):
+    design, observed, filter_taps = arrays[0], arrays[1], arrays[4]
+    sizes = (lax.axis_size("tm"), lax.axis_size("coef"), *design.shape, observed.shape[1], filter_taps.shape[0])
+    return fused_shards(*arrays) if fits(*sizes) else general_shards(*arrays)
+
+
 def solution(mesh):
     placed = (P("tm", "coef"), P("tm", None), P("tm"), P("tm"), P(), P("coef"), P("coef"))
     return jax.shard_map(

time: 510 us -> 211 us (0.41)
  waiting for transfers between devices: 409 us -> 0 us
  Pallas kernels: 0 us -> 202 us
  matrix products: 33.9 us -> 0 us
  local copies, waits for them, and re-layouts: 31.5 us -> 5.72 us
  between operations: 14.8 us -> 1.3 us
  other arithmetic: 11.1 us -> 0 us
  starting transfers between devices: 7.75 us -> 0 us
    psum x2 -> x0, waiting for transfers between devices: 259 us -> none  [summed(): total = lax.psum(jnp.concatenate([partial] + rows, 0), ('tm', 'coef'))]
    pallas_call x0 -> x1, Pallas kernels: none -> 202 us  [fused_shards(): pl.pallas_call(functools.partial(fused, plan), out_shape=(shape, shape),...]
    all_gather x1 -> x0, waiting for transfers between devices: 150 us -> none  [shards(): gathered = lax.all_gather(packed, 'tm', axis=0, tiled=False)]
    dot_general x17 -> x0, matrix products: 33.9 us -> none  [the longest x3 12.8 us: transposed(): lax.dot_general(block, filtered, (((0,), (0,)), ((), ())), preferred_elem...]
    all_to_all x1 -> x0, starting transfers between devices: 7.45 us -> none  [shards(): lax.all_to_all(design, 'tm', split_axis=1, concat_axis=0, tiled=True)]
    unnamed x41 -> x10, local copies, waits for them, and re-layouts: 10.8 us -> 3.85 us
  transfers between devices with their start and end apart: 4 -> 0, of which waited for: 3 -> 0; matrix products, arithmetic and copies ran while one was open for 2% -> 0% of each run, Pallas kernels for 0% -> 0%
where the time goes in v2:
time: 211 us; the launch traced here: 209 us
  Pallas kernels  202 us (96%)
  local copies, waits for them, and re-layouts  5.72 us (3%)
    pallas_call x1, Pallas kernels, fused_shards(): pl.pallas_call(functools.partial(fused, plan), out_shape=(shape, shape),...  202 us

profile of v2, /device:TPU:0, one launch (start us, length us, event | category | flops | bytes accessed | tf_op | source)
XLA Modules:
  0.0 208.7 jit_solution(8035219469069782562)
XLA Ops:
  1.3 0.0 copy-start
  1.3 0.9 copy-done
  2.2 0.0 copy-start.1
  2.2 0.8 copy-done.1
  3.0 0.0 copy-start.2
  3.0 0.8 copy-done.2
  3.8 0.0 copy-start.3
  3.8 0.7 copy-done.3
  4.5 0.0 copy-start.4
  4.5 0.7 copy-done.4
  5.1 201.7 %shard_map.86 = (f32[1792,128]{1,0:T(8,128)S(1)}, f32[1792,128]{1,0:T(8,128)S(1)}) custom-call(bf16[256,12544]{1,0:T(8,128)(2,1)} %design.1, f32[256,128]{1,0:T(8,128)S(1)} %copy-done, s32[2,128]{1,0:T(2,128)S(1)} %bitcast.6, s32[1]{0:T(128)S(6)} %copy.9.counts, f32[1,128]{1,0:T(1,128)S(1)} %bitcast.7, f32[98,128]{1,0:T(8,128)S(1)} %bitcast.4, ...), custom_call_target="tpu_custom_call" | custom-call | tf_op jit(solution)/shard_map/pallas_call | solution.py:635
  206.8 0.9 slice.6
  207.8 0.9 slice.7
Async XLA Ops:
  1.3 0.9 copy-start
  2.2 0.8 copy-start.1
  3.0 0.8 copy-start.2
  3.8 0.7 copy-start.3
  4.5 0.7 copy-start.4

commit v3 on v2

--- a/solution.py
+++ b/solution.py
@@ -180,9 +180,9 @@
 
 def fused(plan, design, observed_in, gap_in, counts, taps_in, kaula_in, precond_in, solution_out, residual_out,
           observed, gap, taps, kaula, precond,
-          block, edges, packed, loose, shown, seen, early, sums, received, total, sent, folded_in, sent_terms, terms_in,
+          block, turned_block, edges, packed, loose, shown, seen, early, sums, received, total, sent, folded_in, sent_terms, terms_in,
           whole, folded, filtered, gathered, resid, direc, scal, solut, first_values,
-          own_sem, small_sem, edge_sem, block_send, block_recv, show_send, show_recv, early_send, early_recv,
+          own_sem, small_sem, edge_sem, block_send, block_recv, loose_recv, show_send, show_recv, early_send, early_recv,
           early_relay_send, early_relay_recv, pair_send, pair_recv, fold_send, fold_recv, term_send, term_recv,
           whole_send, whole_recv, gather_send, gather_recv, relay_send, relay_recv):
     slabs, chips, rows = plan.slabs, plan.chips, plan.epoch_rows
@@ -231,14 +231,12 @@
         design.at[:, tile_columns(first + 1, plan.mixed_at)], block.at[slab, :, pl.ds(0, plan.mixed_at)], own_sem
     )
     own.start()
-    edge_copies = []
     for owner in range(slabs):
         begin = owner * plan.owned // LANES
         for at, tile in enumerate((begin, begin + plan.full + 1)):
-            edge_copies.append(pltpu.make_async_copy(
-                design.at[:, pl.ds(tile * LANES, LANES)], edges.at[owner, at], edge_sem.at[owner, at]
-            ))
-            edge_copies[-1].start()
+            pltpu.make_async_copy(
+                design.at[:, pl.ds(tile * LANES, LANES)], edges.at[owner, at], edge_sem
+            ).start()
 
     for copy in small[:3]:
         copy.wait()
@@ -262,29 +260,23 @@
             src, dst = packed.at[peer, pl.ds(0, rows)], block.at[slab, :, pl.ds(plan.mixed_at, LANES)]
         else:
             src, dst = packed.at[peer, pl.ds(rows, plan.packed_rows)], loose.at[slab]
-        return remote(src, dst, block_send.at[part, peer], block_recv.at[part, slab], {"tm": peer, "coef": coef})
+        return remote(src, dst, block_send.at[part], loose_recv if part == 3 else block_recv.at[min(part, 1), slab], {"tm": peer, "coef": coef})
 
     def block_arrival(bits, part):
         peer = flipped(slab, bits, slabs)
-        if part == 0:
-            dst = block.at[peer, :, pl.ds(0, plan.cut)]
-        elif part == 1:
-            dst = block.at[peer, :, pl.ds(plan.cut, plan.mixed_at - plan.cut)]
-        elif part == 2:
-            dst = block.at[peer, :, pl.ds(plan.mixed_at, LANES)]
-        else:
-            dst = loose.at[peer]
-        return remote(dst, dst, block_send.at[part, peer], block_recv.at[part, peer], {"tm": peer, "coef": coef})
+        low, size = ((0, plan.cut), (plan.cut, plan.mixed_at + LANES - plan.cut))[part]
+        dst = block.at[peer, :, pl.ds(low, size)]
+        return remote(dst, dst, block_send.at[part], block_recv.at[part, peer], {"tm": peer, "coef": coef})
+
+    def all_of(ref, send, recv):
+        return remote(ref, ref, send, recv, partner)
 
     def show_copy(bits):
         peer = flipped(slab, bits, slabs)
         src = shown.at[2 * lax.rem(peer * plan.across + across, half_chips) + core]
-        return remote(src, seen.at[slab], show_send.at[peer], show_recv.at[slab], {"tm": peer, "coef": coef})
-
-    def show_arrival(bits):
-        peer = flipped(slab, bits, slabs)
-        return remote(seen.at[peer], seen.at[peer], show_send.at[peer], show_recv.at[peer], {"tm": peer, "coef": coef})
-
+        return remote(src, seen.at[slab], show_send, show_recv, {"tm": peer, "coef": coef})
+
+    others = pl.ds(0, slabs - 1)
     pl.semaphore_wait(barrier, chips)
     for bits in range(1, slabs):
         show_copy(bits).start()
@@ -294,8 +286,7 @@
     for bits in range(half_slabs, slabs):
         block_copy(bits, 0).start()
 
-    for copy in edge_copies:
-        copy.wait()
+    pltpu.make_async_copy(edges, edges, edge_sem).wait()
     lane_row = lax.broadcasted_iota(jnp.int32, (1, LANES), 1)
     for owner in range(slabs):
         skip = owner * plan.owned % LANES
@@ -313,24 +304,22 @@
         block_copy(bits, 2).start()
         block_copy(bits, 3).start()
 
-    def unpack(at):
-        tight = loose[at].astype(jnp.float32)
+    def unpack(at, tight):
+        tight = tight.astype(jnp.float32)
         for piece in range(LANES // plan.rest):
             part = pltpu.roll(tight, LANES - piece * plan.rest, 1) if piece else tight
             part = jnp.where(lane_row < plan.rest, part, 0.0).astype(jnp.bfloat16)
             block[at, piece * plan.packed_rows:(piece + 1) * plan.packed_rows, plan.mixed_at + LANES:] = part
 
     block[slab, :, plan.mixed_at:plan.mixed_at + LANES] = packed[slab, :rows]
-    loose[slab] = packed[slab, rows:]
-    unpack(slab)
+    unpack(slab, packed[slab, rows:])
 
     base = jnp.concatenate([taps[...], jnp.zeros((1, LANES), jnp.float32)], 1)
     shifted = pltpu.roll(jnp.broadcast_to(base, (LANES, 2 * LANES)), 0, 1, stride=1, stride_axis=0)
     lower, upper = shifted[:, :LANES], shifted[:, LANES:]
     blank = jnp.zeros((GROUP, LANES), jnp.float32)
 
-    for bits in range(1, slabs):
-        show_arrival(bits).wait_recv()
+    all_of(seen.at[others], show_send, show_recv).wait_recv()
 
     def stack(ref, low):
         return jnp.concatenate(
@@ -354,7 +343,7 @@
         to = near_other(step)
         here = early.at[core, near_chip]
         target = device(this_half * half_chips + to)
-        remote(here, here, early_send.at[to], early_recv.at[near_chip], target).start()
+        remote(here, here, early_send, early_recv, target).start()
     for bits in range(half_slabs, slabs):
         block_copy(bits, 1).start()
 
@@ -370,13 +359,8 @@
 
     ridge_row, scale_row = local_row(kaula), local_row(precond)
 
-    def early_arrival(step):
-        at = near_other(step)
-        here = early.at[core, at]
-        return remote(here, here, early_send.at[at], early_recv.at[at], device(this_half * half_chips + at))
-
-    for step in range(1, half_chips):
-        early_arrival(step).wait_recv()
+    near_others = pl.ds(0, half_chips - 1)
+    all_of(early.at[core, near_others], early_send, early_recv).wait_recv()
     mine, theirs = early.at[core], early.at[1 - core]
     remote(mine, mine, early_relay_send, early_relay_recv, partner).start()
     remote(theirs, theirs, early_relay_send, early_relay_recv, partner).wait_recv()
@@ -393,46 +377,47 @@
 
     own.wait()
     spans = (slice(0, plan.cut), slice(plan.cut, plan.width))
+
+    def turn_over(at, span):
+        turned_block[at, span] = block[at, :, span].T
+
     for part, span in enumerate(spans):
+        if part:
+            all_of(loose.at[others], block_send.at[3], loose_recv).wait_recv()
+        turn_over(slab, span)
         resid[:, span] = product(series(slab), block[slab, :, span], NN)
         for bits in range(1, slabs):
             peer = flipped(slab, bits, slabs)
-            for piece in ((0,), (1, 2, 3))[part]:
-                block_arrival(bits, piece).wait_recv()
+            block_arrival(bits, part).wait_recv()
             if part:
-                unpack(peer)
+                unpack(peer, loose[peer])
+            turn_over(peer, span)
             resid[:, span] += product(series(peer), block[peer, :, span], NN)
         direc[:, span] = scale_row[:, span] * resid[:, span]
         if part == 0:
             low = direc[:, span].astype(jnp.bfloat16)
 
             def body(at, carry):
-                sums[0, at] = product(low, block[at, :, :plan.cut], NT)
+                sums[0, at] = product(low, turned_block[at, :plan.cut], NN)
                 return carry
 
             lax.fori_loop(0, slabs, body, 0)
 
     def pair_copy(turn, j):
         src = sums.at[turn, (1 - core) * half_slabs + j]
-        return remote(src, received.at[turn, j], pair_send.at[turn, j], pair_recv.at[turn, j], partner)
+        return remote(src, received.at[turn, j], pair_send.at[turn], pair_recv.at[turn, j], partner)
 
     def fold_copy(turn, j, step):
         to = other(step)
         src, dst = sent.at[turn, j, to], folded_in.at[turn, j, chip]
-        return remote(src, dst, fold_send.at[turn, j, to], fold_recv.at[turn, j, chip], device(to))
-
-    def fold_arrival(turn, j, at):
-        here = folded_in.at[turn, j, at]
-        return remote(here, here, fold_send.at[turn, j, at], fold_recv.at[turn, j, at], device(at))
+        return remote(src, dst, fold_send.at[turn], fold_recv.at[turn, j], device(to))
+
+    other_chips = pl.ds(0, chips - 1)
 
     def term_copy(turn, step):
         to = other(step)
         src, dst = sent_terms.at[turn, to], terms_in.at[turn, chip]
-        return remote(src, dst, term_send.at[turn, to], term_recv.at[turn, chip], device(to))
-
-    def term_arrival(turn, at):
-        here = terms_in.at[turn, at]
-        return remote(here, here, term_send.at[turn, at], term_recv.at[turn, at], device(at))
+        return remote(src, dst, term_send.at[turn], term_recv.at[turn], device(to))
 
     def each_chip(action):
         def body(step, carry):
@@ -448,7 +433,7 @@
         each_chip(lambda step: term_copy(turn, step).start())
 
         def partial(at):
-            value = product(low, block[at, :, span], NT)
+            value = product(low, turned_block[at, span], NN)
             return value + sums[turn, at] if turn == 0 else value
 
         def give(j, carry):
@@ -470,19 +455,17 @@
 
         lax.fori_loop(0, half_slabs, keep, 0)
 
-        def take(step, carry):
-            at = other(step)
-            term_arrival(turn, at).wait_recv()
-            return carry + terms_in[turn, at].astype(jnp.float32)
-
-        whole[turn, core, :, plan.half:] = lax.fori_loop(1, chips, take, terms_in[turn, chip].astype(jnp.float32))
+        def added(ref, start):
+            def body(step, carry):
+                return carry + ref[other(step)].astype(jnp.float32)
+
+            return lax.fori_loop(1, chips, body, start, unroll=True)
+
+        all_of(terms_in.at[turn, other_chips], term_send.at[turn], term_recv.at[turn]).wait_recv()
+        whole[turn, core, :, plan.half:] = added(terms_in.at[turn], terms_in[turn, chip].astype(jnp.float32))
         for j in range(half_slabs):
-            def arrive(step, carry):
-                at = other(step)
-                fold_arrival(turn, j, at).wait_recv()
-                return carry + folded_in[turn, j, at].astype(jnp.float32)
-
-            whole[turn, core, :, j * rows:(j + 1) * rows] = lax.fori_loop(1, chips, arrive, total[j, chip])
+            all_of(folded_in.at[turn, j, other_chips], fold_send.at[turn], fold_recv.at[turn, j]).wait_recv()
+            whole[turn, core, :, j * rows:(j + 1) * rows] = added(folded_in.at[turn, j], total[j, chip])
         mine, theirs = whole.at[turn, core], whole.at[turn, 1 - core]
         remote(mine, mine, whole_send.at[turn], whole_recv.at[turn], partner).start()
         remote(theirs, theirs, whole_send.at[turn], whole_recv.at[turn], partner).wait_recv()
@@ -493,21 +476,12 @@
         return values, [joined(scalars, at) for at in range(len(terms))]
 
     def gather_copy(phase, step):
-        to = other(step)
         here = gathered.at[phase, core, chip]
-        return remote(here, here, gather_send.at[phase, to], gather_recv.at[phase, chip], device(to))
-
-    def gather_arrival(phase, at):
-        here = gathered.at[phase, core, at]
-        return remote(here, here, gather_send.at[phase, at], gather_recv.at[phase, at], device(at))
-
-    def relay_copy(phase, at):
-        here = gathered.at[phase, core, at]
-        return remote(here, here, relay_send.at[phase, at], relay_recv.at[phase, at], partner)
-
-    def relay_arrival(phase, at):
-        here = gathered.at[phase, 1 - core, at]
-        return remote(here, here, relay_send.at[phase, at], relay_recv.at[phase, at], partner)
+        return remote(here, here, gather_send.at[phase], gather_recv.at[phase], device(other(step)))
+
+    def relay_copy(phase, which):
+        here = gathered.at[phase, which]
+        return remote(here, here, relay_send.at[phase], relay_recv.at[phase], partner)
 
     def shared(phase, values, terms):
         wide = values.astype(jnp.float32)
@@ -518,16 +492,9 @@
             folded[half, :, plan.half:] = pieces(in_lanes(terms, GROUP))
         gathered[phase, core, chip] = folded[core].astype(jnp.bfloat16)
         each_chip(lambda step: gather_copy(phase, step).start())
-        relay_copy(phase, chip).start()
-
-        def pass_on(step):
-            at = other(step)
-            gather_arrival(phase, at).wait_recv()
-            relay_copy(phase, at).start()
-
-        each_chip(pass_on)
-        relay_arrival(phase, chip).wait_recv()
-        each_chip(lambda step: relay_arrival(phase, other(step)).wait_recv())
+        all_of(gathered.at[phase, core, other_chips], gather_send.at[phase], gather_recv.at[phase]).wait_recv()
+        relay_copy(phase, core).start()
+        relay_copy(phase, 1 - core).wait_recv()
         for half in range(2):
             for j in range(half_slabs):
                 part = gathered[phase, half, :, :, j * rows:(j + 1) * rows].astype(jnp.float32)
@@ -573,7 +540,7 @@
     step_col, ratio_col = shared(1, kept, [step_len, ratio])
 
     def put(out, tile, value):
-        out[pl.ds(pl.multiple_of((tile + 2) * LANES - offset, plan.rest), LANES), :] = value
+        out[(tile + 1) * LANES:(tile + 2) * LANES, :] = value
 
     held = {}
     for span in chunks:
@@ -586,37 +553,30 @@
             new_ahead, new_left = held.pop(tile)
             put(solution_out, tile, new_ahead)
             put(residual_out, tile, new_left)
-    mixed = held[plan.full]
-    last = held[plan.full + 1]
-    for out, first_value, second in ((solution_out, mixed[0], last[0]), (residual_out, mixed[1], last[1])):
-        low = pl.multiple_of(LANES - offset, plan.rest)
-        out[pl.ds(low, LANES), :] = first_value
-        low = pl.multiple_of((plan.full + 2) * LANES - offset, plan.rest)
-        out[pl.ds(low, LANES), :] = first_value
-        low = (plan.full + 2) * LANES
-        out[low:low + plan.rest, :] = second[:plan.rest]
-
-    for bits in range(1, slabs):
-        show_copy(bits).wait_send()
-        for part in range(4):
-            block_copy(bits, part).wait_send()
-    for step in range(1, half_chips):
-        to = near_other(step)
-        here = early.at[core, near_chip]
-        target = device(this_half * half_chips + to)
-        remote(here, here, early_send.at[to], early_recv.at[near_chip], target).wait_send()
-    mine = early.at[core]
-    remote(mine, mine, early_relay_send, early_relay_recv, partner).wait_send()
+    mixed, last = held[plan.full], held[plan.full + 1]
+    for out, edge, end in ((solution_out, mixed[0], last[0]), (residual_out, mixed[1], last[1])):
+        out[:LANES, :] = edge
+        put(out, plan.full, edge)
+        low = pl.multiple_of((plan.full + 1) * LANES + offset, plan.rest)
+        out[pl.ds(low, plan.rest), :] = end[:plan.rest]
+
+    all_of(shown.at[others], show_send, show_recv).wait_send()
+    for part, (low, size) in enumerate(((0, plan.cut), (plan.cut, plan.mixed_at - plan.cut), (plan.mixed_at, LANES))):
+        all_of(block.at[others, :, pl.ds(low, size)], block_send.at[part], loose_recv).wait_send()
+    all_of(loose.at[others], block_send.at[3], loose_recv).wait_send()
+    all_of(early.at[core, near_others], early_send, early_recv).wait_send()
+    all_of(early.at[core], early_relay_send, early_relay_recv).wait_send()
     for turn in range(2):
-        for j in range(half_slabs):
-            pair_copy(turn, j).wait_send()
-            each_chip(lambda step: fold_copy(turn, j, step).wait_send())
-        each_chip(lambda step: term_copy(turn, step).wait_send())
-        mine = whole.at[turn, core]
-        remote(mine, mine, whole_send.at[turn], whole_recv.at[turn], partner).wait_send()
-        each_chip(lambda step: gather_copy(turn, step).wait_send())
-        relay_copy(turn, chip).wait_send()
-        each_chip(lambda step: relay_copy(turn, other(step)).wait_send())
+        all_of(received.at[turn], pair_send.at[turn], pair_recv.at[turn, 0]).wait_send()
+        all_of(sent.at[turn, :, other_chips], fold_send.at[turn], fold_recv.at[turn, 0]).wait_send()
+        all_of(sent_terms.at[turn, other_chips], term_send.at[turn], term_recv.at[turn]).wait_send()
+        all_of(whole.at[turn, core], whole_send.at[turn], whole_recv.at[turn]).wait_send()
+        all_of(gathered.at[turn, core, other_chips], gather_send.at[turn], gather_recv.at[turn]).wait_send()
+        all_of(gathered.at[turn, core], relay_send.at[turn], relay_recv.at[turn]).wait_send()
+
+
+def far(value):
+    return pltpu.with_memory_space_constraint(value, pltpu.HBM)
 
 
 def fused_shards(design, observed, slab_counts, gap_mask, filter_taps, kaula_diag, precond):
@@ -644,6 +604,7 @@
             pltpu.VMEM(tiles, f32),
             pltpu.VMEM(tiles, f32),
             pltpu.VMEM((slabs, epoch_rows, wide), bf16),
+            pltpu.VMEM((slabs, wide, epoch_rows), bf16),
             pltpu.VMEM((slabs, 2, epoch_rows, LANES), bf16),
             pltpu.VMEM((slabs, epoch_rows + plan.packed_rows, LANES), bf16),
             pltpu.VMEM((slabs, plan.packed_rows, LANES), bf16),
@@ -666,20 +627,21 @@
             pltpu.VMEM((columns, wide), f32),
             pltpu.VMEM((columns, wide), f32),
             pltpu.VMEM((plan.blocks * GROUP, LANES), f32),
-            sem(()), sem((5,)), sem((slabs, 2)), sem((4, slabs)), sem((4, slabs)), sem((slabs,)), sem((slabs,)),
-            sem((half_chips,)), sem((half_chips,)), sem(()), sem(()),
-            sem((2, half_slabs)), sem((2, half_slabs)), sem((2, half_slabs, chips)), sem((2, half_slabs, chips)),
-            sem((2, chips)), sem((2, chips)), sem((2,)), sem((2,)),
-            sem((2, chips)), sem((2, chips)), sem((2, chips)), sem((2, chips)),
+            sem(()), sem((5,)), sem(()), sem((4,)), sem((2, slabs)), sem(()), sem(()), sem(()),
+            sem(()), sem(()), sem(()), sem(()),
+            sem((2,)), sem((2, half_slabs)), sem((2,)), sem((2, half_slabs)), sem((2,)), sem((2,)), sem((2,)), sem((2,)),
+            sem((2,)), sem((2,)), sem((2,)), sem((2,)),
         ],
         compiler_params=pltpu.CompilerParams(
             collective_id=0, has_side_effects=True, vmem_limit_bytes=48 * 1024 * 1024
         ),
     )(
-        design, observed, gap_mask.reshape(-1, LANES), slab_counts, filter_taps[None],
-        kaula_diag.reshape(tiles), precond.reshape(tiles),
+        design, far(observed), far(gap_mask.reshape(-1, LANES)), slab_counts, far(filter_taps[None]),
+        far(kaula_diag.reshape(tiles)), far(precond.reshape(tiles)),
     )
-    return tuple(out[LANES:LANES + plan.owned] for out in outs)
+    owner = lax.axis_index("tm")
+    low = owner * plan.owned - plan.first_tile(owner) * LANES
+    return tuple(lax.dynamic_slice_in_dim(out, low, plan.owned, 0) for out in outs)
 
 
 def shards(*arrays):

time: 211 us -> 198 us (0.938)
  Pallas kernels: 202 us -> 194 us
  local copies, waits for them, and re-layouts: 5.72 us -> 1.26 us
    pallas_call x1, Pallas kernels: 202 us -> 194 us  [fused_shards(): pl.pallas_call(functools.partial(fused, plan), out_shape=(shape, shape),...]
    unnamed x10 -> x0, local copies, waits for them, and re-layouts: 3.85 us -> none
where the time goes in v3:
time: 198 us; the launch traced here: 196 us
  Pallas kernels  194 us (98%)
    pallas_call x1, Pallas kernels, fused_shards(): pl.pallas_call(functools.partial(fused, plan), out_shape=(shape, shape),...  194 us

profile of v3, /device:TPU:0, one launch (start us, length us, event | category | flops | bytes accessed | tf_op | source)
XLA Modules:
  0.0 196.5 jit_solution(14742814209231058108)
XLA Ops:
  1.3 193.9 %shard_map.86 = (f32[1792,128]{1,0:T(8,128)S(1)}, f32[1792,128]{1,0:T(8,128)S(1)}) custom-call(bf16[256,12544]{1,0:T(8,128)(2,1)} %design.1, f32[256,128]{1,0:T(8,128)} %observed_in.1, s32[2,128]{1,0:T(2,128)} %bitcast.6, s32[1]{0:T(128)S(6)} %copy.9.counts, f32[1,128]{1,0:T(1,128)} %bitcast.7, f32[98,128]{1,0:T(8,128)} %bitcast.4, f32[98,128]{1,0:T(8,128)} %bitcast.5), custom_call_target="tpu_custom_call" | custom-call | tf_op jit(solution)/shard_map/pallas_call | solution.py:595
  195.2 1.3 constant_dynamic-slice_fusion

commit v4 on v3

--- a/solution.py
+++ b/solution.py
@@ -120,12 +120,15 @@
         self.packed_rows = epoch_rows * self.rest // LANES
         self.mixed_at = self.full * LANES
         self.width = (self.full + 2) * LANES
-        self.cut = self.full * 3 // 4 * LANES
+        self.cut = (self.full - 1) * LANES
         self.across = coefs // 2
         self.chips = slabs * self.across
         self.blocks = slabs * epoch_rows // LANES
-        self.half = slabs * epoch_rows // 2
-        self.message = self.half + LANES
+        self.half_blocks = self.blocks // 2
+        per_slab, half_slabs = epoch_rows // LANES, slabs // 2
+        ends = [(upto + 1) * per_slab - 1 for upto in range(1, half_slabs - 1)] + [self.half_blocks]
+        self.groups = list(zip([0] + ends[:-1], ends))
+        self.message = LANES * (1 + max(end - begin for begin, end in self.groups))
 
     def first_tile(self, owner):
         return lax.div(owner * self.owned, LANES)
@@ -181,12 +184,12 @@
 def fused(plan, design, observed_in, gap_in, counts, taps_in, kaula_in, precond_in, solution_out, residual_out,
           observed, gap, taps, kaula, precond,
           block, turned_block, edges, packed, loose, shown, seen, early, sums, received, total, sent, folded_in, sent_terms, terms_in,
-          whole, folded, filtered, gathered, resid, direc, scal, solut, first_values,
+          whole, entering, weights, filtered, gathered, resid, direc, scal, solut, first_values,
           own_sem, small_sem, edge_sem, block_send, block_recv, loose_recv, show_send, show_recv, early_send, early_recv,
           early_relay_send, early_relay_recv, pair_send, pair_recv, fold_send, fold_recv, term_send, term_recv,
-          whole_send, whole_recv, gather_send, gather_recv, relay_send, relay_recv):
+          whole_send, whole_recv, middle_send, middle_recv, gather_send, gather_recv, relay_send, relay_recv):
     slabs, chips, rows = plan.slabs, plan.chips, plan.epoch_rows
-    half_slabs, half_chips, half_blocks = slabs // 2, chips // 2, plan.blocks // 2
+    half_slabs, half_chips, half_blocks = slabs // 2, chips // 2, plan.half_blocks
     slab, coef = lax.axis_index("tm"), lax.axis_index("coef")
     across, core = lax.div(coef, 2), lax.rem(coef, 2)
     chip = slab * plan.across + across
@@ -336,6 +339,24 @@
         outer = product(inner, lower, NT, lax.Precision.HIGHEST) + product(after, upper, NT, lax.Precision.HIGHEST)
         return (weight * outer).astype(jnp.bfloat16)
 
+    def nearer(span):
+        parts = [span[:, at * LANES:(at + 1) * LANES] for at in range(rows // LANES)]
+        return [jnp.where(core == 0, left, right) for left, right in zip(parts[::-1], parts)]
+
+    def outward(at, which):
+        return which * (half_slabs + at) + (1 - which) * (half_slabs - 1 - at)
+
+    for at in range(half_slabs):
+        for j, part in enumerate(nearer(seen[outward(at, core), GROUP:, :])):
+            weights[at * (rows // LANES) + j] = part
+    exact = lax.Precision.HIGHEST
+    ends_block = product(lower, lower, NT, exact)
+    same_block = ends_block + product(upper, upper, NT, exact)
+    before_block, after_block = product(upper, lower, NT, exact), product(lower, upper, NT, exact)
+    inside_block = jnp.where(core == 0, after_block, before_block)
+    outside_block = jnp.where(core == 0, before_block, after_block)
+    ends_block = jnp.where(core == 0, same_block, ends_block)
+
     kept = weighted(stack(seen, 0)).astype(jnp.float32)
     for j in range(plan.blocks):
         early[core, near_chip, :, j * LANES:(j + 1) * LANES] = kept[j * GROUP:(j + 1) * GROUP].astype(jnp.bfloat16)
@@ -404,7 +425,7 @@
             lax.fori_loop(0, slabs, body, 0)
 
     def pair_copy(turn, j):
-        src = sums.at[turn, (1 - core) * half_slabs + j]
+        src = sums.at[turn, outward(j, 1 - core)]
         return remote(src, received.at[turn, j], pair_send.at[turn], pair_recv.at[turn, j], partner)
 
     def fold_copy(turn, j, step):
@@ -420,13 +441,13 @@
         return remote(src, dst, term_send.at[turn], term_recv.at[turn], device(to))
 
     def each_chip(action):
-        def body(step, carry):
-            action(step)
+        def body(at, carry):
+            action(half_chips + (1 - 2 * lax.rem(at, 2)) * lax.div(at + 1, 2))
             return carry
 
-        lax.fori_loop(1, chips, body, 0)
-
-    def summed(turn, low, terms, span):
+        lax.fori_loop(0, chips - 1, body, 0)
+
+    def filtered_sum(turn, low, terms, span, settle):
         scalars = in_lanes(terms, plan.columns)
         sent_terms[turn] = pieces(scalars).reshape(chips, GROUP, LANES).astype(jnp.bfloat16)
         terms_in[turn, chip] = sent_terms[turn, chip]
@@ -436,24 +457,27 @@
             value = product(low, turned_block[at, span], NN)
             return value + sums[turn, at] if turn == 0 else value
 
-        def give(j, carry):
-            at = (1 - core) * half_slabs + j
+        def give(j):
+            at = outward(j, 1 - core)
             sums[turn, at] = partial(at)
             pair_copy(turn, j).start()
-            return carry
-
-        lax.fori_loop(0, half_slabs, give, 0)
-
-        def keep(j, carry):
-            value = partial(core * half_slabs + j)
+
+        def keep(j):
+            value = partial(outward(j, core))
             pair_copy(turn, j).wait_recv()
             value = (value + received[turn, j]).reshape(chips, GROUP, rows)
             total[j] = value
             sent[turn, j] = value.astype(jnp.bfloat16)
             each_chip(lambda step: fold_copy(turn, j, step).start())
+
+        def both(j, carry):
+            give(j + 1)
+            keep(j)
             return carry
 
-        lax.fori_loop(0, half_slabs, keep, 0)
+        give(0)
+        lax.fori_loop(0, half_slabs - 1, both, 0)
+        keep(half_slabs - 1)
 
         def added(ref, start):
             def body(step, carry):
@@ -462,50 +486,91 @@
             return lax.fori_loop(1, chips, body, start, unroll=True)
 
         all_of(terms_in.at[turn, other_chips], term_send.at[turn], term_recv.at[turn]).wait_recv()
-        whole[turn, core, :, plan.half:] = added(terms_in.at[turn], terms_in[turn, chip].astype(jnp.float32))
-        for j in range(half_slabs):
-            all_of(folded_in.at[turn, j, other_chips], fold_send.at[turn], fold_recv.at[turn, j]).wait_recv()
-            whole[turn, core, :, j * rows:(j + 1) * rows] = added(folded_in.at[turn, j], total[j, chip])
+        whole[turn, core] = added(terms_in.at[turn], terms_in[turn, chip].astype(jnp.float32))
         mine, theirs = whole.at[turn, core], whole.at[turn, 1 - core]
         remote(mine, mine, whole_send.at[turn], whole_recv.at[turn], partner).start()
         remote(theirs, theirs, whole_send.at[turn], whole_recv.at[turn], partner).wait_recv()
-        values = jnp.concatenate(
-            [whole[turn, half, :, j * LANES:(j + 1) * LANES] for half in range(2) for j in range(half_blocks)], 0
-        )
-        scalars = whole[turn, 0, :, plan.half:] + whole[turn, 1, :, plan.half:]
-        return values, [joined(scalars, at) for at in range(len(terms))]
-
-    def gather_copy(phase, step):
-        here = gathered.at[phase, core, chip]
-        return remote(here, here, gather_send.at[phase], gather_recv.at[phase], device(other(step)))
-
-    def relay_copy(phase, which):
-        here = gathered.at[phase, which]
-        return remote(here, here, relay_send.at[phase], relay_recv.at[phase], partner)
-
-    def shared(phase, values, terms):
-        wide = values.astype(jnp.float32)
-        for half in range(2):
-            for j in range(half_blocks):
-                low = (half * half_blocks + j) * GROUP
-                folded[half, :, j * LANES:(j + 1) * LANES] = wide[low:low + GROUP]
-            folded[half, :, plan.half:] = pieces(in_lanes(terms, GROUP))
-        gathered[phase, core, chip] = folded[core].astype(jnp.bfloat16)
-        each_chip(lambda step: gather_copy(phase, step).start())
-        all_of(gathered.at[phase, core, other_chips], gather_send.at[phase], gather_recv.at[phase]).wait_recv()
-        relay_copy(phase, core).start()
-        relay_copy(phase, 1 - core).wait_recv()
-        for half in range(2):
-            for j in range(half_slabs):
-                part = gathered[phase, half, :, :, j * rows:(j + 1) * rows].astype(jnp.float32)
-                low = half * plan.half + j * rows
-                filtered[:, low:low + rows] = part.reshape(plan.columns, rows).astype(jnp.bfloat16)
-        scalars = gathered[phase, 0, :, :, plan.half:].astype(jnp.float32).reshape(plan.columns, LANES)
-        return [joined(scalars, at) for at in range(len(terms))]
-
-    def inner(left, right):
-        together = (left * right).reshape(plan.blocks, GROUP, LANES)
-        return over(jnp.sum(together, 0))
+        scalars = whole[turn, 0] + whole[turn, 1]
+        scalars = [joined(scalars, at) for at in range(len(terms))]
+        ratio, more = settle(scalars)
+
+        per_slab = rows // LANES
+        overlap = jnp.zeros((GROUP, LANES), jnp.float32)
+        group = 0
+        entering[turn, half_blocks + 1] = blank
+        for j in range(half_slabs):
+            all_of(folded_in.at[turn, j, other_chips], fold_send.at[turn], fold_recv.at[turn, j]).wait_recv()
+            for at, value in enumerate(nearer(added(folded_in.at[turn, j], total[j, chip]))):
+                at = j * per_slab + at
+                if ratio is not None:
+                    value = value + ratio * first_values[0, at]
+                first_values[turn, at] = value
+                entering[turn, at + 1] = weights[at] * value
+            if j == 0:
+                middle_copy(turn, 1).start()
+                continue
+            if j == 1:
+                middle_copy(turn, 0).wait_recv()
+            begin, end = plan.groups[group]
+            count = end - begin
+
+            def rows_of(ref):
+                return ref.reshape(count * GROUP, LANES)
+
+            here = rows_of(entering[turn, begin + 1:end + 1])
+            outer = product(rows_of(entering[turn, begin:end]), inside_block, NN, exact)
+            outer = outer + product(rows_of(entering[turn, begin + 2:end + 2]), outside_block, NN, exact)
+            if end == half_blocks:
+                kept = jnp.concatenate([
+                    product(here[:-GROUP], same_block, NN, exact), product(here[-GROUP:], ends_block, NN, exact)
+                ], 0)
+            else:
+                kept = product(here, same_block, NN, exact)
+            kept = (rows_of(weights[begin:end]) * (outer + kept)).astype(jnp.bfloat16).astype(jnp.float32)
+            with_values = rows_of(first_values[turn, begin:end]) * kept
+            overlap = overlap + jnp.sum(with_values.reshape(count, GROUP, LANES), 0)
+            parts = [kept[at * GROUP:(at + 1) * GROUP] for at in range(count)]
+            if end == half_blocks:
+                parts.append(pieces(in_lanes([over(overlap)] + more, GROUP)))
+            gathered[turn, group, core, chip, :, :len(parts) * LANES] = jnp.concatenate(parts, 1).astype(jnp.bfloat16)
+            each_chip(lambda step: gather_copy(turn, group, step).start())
+            group += 1
+        for group in range(len(plan.groups)):
+            everyone = gathered.at[turn, group, core, other_chips, :, pl.ds(0, extent(group))]
+            all_of(everyone, gather_send.at[turn, group], gather_recv.at[turn, group]).wait_recv()
+            relay_copy(turn, group, core).start()
+        for group, (begin, end) in enumerate(plan.groups):
+            relay_copy(turn, group, 1 - core).wait_recv()
+            for half in range(2):
+                for at in range(begin, end):
+                    part = gathered[turn, group, half, :, :, (at - begin) * LANES:(at - begin + 1) * LANES]
+                    part = part.astype(jnp.float32).reshape(plan.columns, LANES).astype(jnp.bfloat16)
+                    low = (half_blocks + at if half else half_blocks - 1 - at) * LANES
+                    filtered[:, low:low + LANES] = part
+        last = len(plan.groups) - 1
+        span = slice(extent(last) - LANES, extent(last))
+        first_terms, second_terms = [
+            gathered[turn, last, half, :, :, span].astype(jnp.float32).reshape(plan.columns, LANES) for half in range(2)
+        ]
+        norm, ridge = joined(first_terms, 1), joined(first_terms, 2)
+        step_col = norm / (ridge + joined(first_terms, 0) + joined(second_terms, 0))
+        return scalars, ratio, step_col, joined(first_terms, 3)
+
+    def extent(group):
+        begin, end = plan.groups[group]
+        return LANES * (end - begin + (end == half_blocks))
+
+    def middle_copy(turn, at):
+        src, dst = entering.at[turn, 1], entering.at[turn, 0]
+        return remote(src if at else dst, dst, middle_send.at[turn], middle_recv.at[turn], partner)
+
+    def gather_copy(turn, group, step):
+        here = gathered.at[turn, group, core, chip, :, pl.ds(0, extent(group))]
+        return remote(here, here, gather_send.at[turn, group], gather_recv.at[turn, group], device(other(step)))
+
+    def relay_copy(turn, group, which):
+        here = gathered.at[turn, group, which, :, :, pl.ds(0, extent(group))]
+        return remote(here, here, relay_send.at[turn, group], relay_recv.at[turn, group], partner)
 
     chunks = [slice(low, min(low + 2 * LANES, plan.width)) for low in range(0, plan.width, 2 * LANES)]
 
@@ -515,11 +580,8 @@
 
     ridged = ridge_row * direc[...]
     terms = [over(resid[...] * direc[...]), over(ridged * direc[...])]
-    values, (norm, ridge) = summed(0, direc[:, spans[1]].astype(jnp.bfloat16), terms, spans[1])
-    first_values[...] = values
-    kept = weighted(values)
-    step_len = norm / (ridge + inner(values, kept.astype(jnp.float32)))
-    (step_col,) = shared(0, kept, [step_len])
+    low = direc[:, spans[1]].astype(jnp.bfloat16)
+    (norm, ridge), _, step_col, _ = filtered_sum(0, low, terms, spans[1], lambda sums_of: (None, list(sums_of)))
     terms = [0.0, 0.0, 0.0]
     for span in chunks:
         along, ridge_part = direc[:, span], ridge_row[:, span]
@@ -531,13 +593,14 @@
         ridged = ridge_part * ahead
         added = (over(left * ahead), over(ridged * ahead), over(ridged * along))
         terms = [term + more for term, more in zip(terms, added)]
-    fresh, (norm_next, own_ridge, cross) = summed(1, scal[...].astype(jnp.bfloat16), terms, slice(0, plan.width))
-    ratio = norm_next / norm
-    ridge = own_ridge + ratio * (2.0 * cross + ratio * ridge)
-    values = fresh + jnp.concatenate([ratio] * plan.blocks, 0) * first_values[...]
-    kept = weighted(values)
-    step_len = norm_next / (ridge + inner(values, kept.astype(jnp.float32)))
-    step_col, ratio_col = shared(1, kept, [step_len, ratio])
+
+    def settle(sums_of):
+        norm_next, own_ridge, cross = sums_of
+        ratio = norm_next / norm
+        return ratio, [norm_next, own_ridge + ratio * (2.0 * cross + ratio * ridge), ratio]
+
+    low = scal[...].astype(jnp.bfloat16)
+    _, _, step_col, ratio_col = filtered_sum(1, low, terms, slice(0, plan.width), settle)
 
     def put(out, tile, value):
         out[(tile + 1) * LANES:(tile + 2) * LANES, :] = value
@@ -571,8 +634,11 @@
         all_of(sent.at[turn, :, other_chips], fold_send.at[turn], fold_recv.at[turn, 0]).wait_send()
         all_of(sent_terms.at[turn, other_chips], term_send.at[turn], term_recv.at[turn]).wait_send()
         all_of(whole.at[turn, core], whole_send.at[turn], whole_recv.at[turn]).wait_send()
-        all_of(gathered.at[turn, core, other_chips], gather_send.at[turn], gather_recv.at[turn]).wait_send()
-        all_of(gathered.at[turn, core], relay_send.at[turn], relay_recv.at[turn]).wait_send()
+        middle_copy(turn, 1).wait_send()
+        for group in range(len(plan.groups)):
+            everyone = gathered.at[turn, group, core, other_chips, :, pl.ds(0, extent(group))]
+            all_of(everyone, gather_send.at[turn, group], gather_recv.at[turn, group]).wait_send()
+            relay_copy(turn, group, core).wait_send()
 
 
 def far(value):
@@ -618,19 +684,20 @@
             pltpu.VMEM((2, half_slabs, chips, GROUP, epoch_rows), bf16),
             pltpu.VMEM((2, chips, GROUP, LANES), bf16),
             pltpu.VMEM((2, chips, GROUP, LANES), bf16),
-            pltpu.VMEM((2, 2, GROUP, message), f32),
-            pltpu.VMEM((2, GROUP, message), f32),
+            pltpu.VMEM((2, 2, GROUP, LANES), f32),
+            pltpu.VMEM((2, plan.half_blocks + 2, GROUP, LANES), f32),
+            pltpu.VMEM((plan.half_blocks, GROUP, LANES), f32),
             pltpu.VMEM((columns, slabs * epoch_rows), bf16),
-            pltpu.VMEM((2, 2, chips, GROUP, message), bf16),
+            pltpu.VMEM((2, len(plan.groups), 2, chips, GROUP, message), bf16),
             pltpu.VMEM((columns, wide), f32),
             pltpu.VMEM((columns, wide), f32),
             pltpu.VMEM((columns, wide), f32),
             pltpu.VMEM((columns, wide), f32),
-            pltpu.VMEM((plan.blocks * GROUP, LANES), f32),
+            pltpu.VMEM((2, plan.half_blocks, GROUP, LANES), f32),
             sem(()), sem((5,)), sem(()), sem((4,)), sem((2, slabs)), sem(()), sem(()), sem(()),
             sem(()), sem(()), sem(()), sem(()),
             sem((2,)), sem((2, half_slabs)), sem((2,)), sem((2, half_slabs)), sem((2,)), sem((2,)), sem((2,)), sem((2,)),
-            sem((2,)), sem((2,)), sem((2,)), sem((2,)),
+            sem((2,)), sem((2,)), *[sem((2, len(plan.groups)))] * 4,
         ],
         compiler_params=pltpu.CompilerParams(
             collective_id=0, has_side_effects=True, vmem_limit_bytes=48 * 1024 * 1024

time: 198 us -> 193 us (0.975)
  Pallas kernels: 194 us -> 190 us
    pallas_call x1, Pallas kernels: 194 us -> 190 us  [fused_shards(): pl.pallas_call(functools.partial(fused, plan), out_shape=(shape, shape),...]
where the time goes in v4:
time: 193 us; the launch traced here: 192 us
  Pallas kernels  190 us (98%)
    pallas_call x1, Pallas kernels, fused_shards(): pl.pallas_call(functools.partial(fused, plan), out_shape=(shape, shape),...  190 us

profile of v4, /device:TPU:0, one launch (start us, length us, event | category | flops | bytes accessed | tf_op | source)
XLA Modules:
  0.0 192.2 jit_solution(9602649132246663295)
XLA Ops:
  1.3 189.6 %shard_map.86 = (f32[1792,128]{1,0:T(8,128)S(1)}, f32[1792,128]{1,0:T(8,128)S(1)}) custom-call(bf16[256,12544]{1,0:T(8,128)(2,1)} %design.1, f32[256,128]{1,0:T(8,128)} %observed_in.1, s32[2,128]{1,0:T(2,128)} %bitcast.6, s32[1]{0:T(128)S(6)} %copy.9.counts, f32[1,128]{1,0:T(1,128)} %bitcast.7, f32[98,128]{1,0:T(8,128)} %bitcast.4, f32[98,128]{1,0:T(8,128)} %bitcast.5), custom_call_target="tpu_custom_call" | custom-call | tf_op jit(solution)/shard_map/pallas_call | solution.py:661
  190.9 1.3 constant_dynamic-slice_fusion

commit v5 on v4

--- a/solution.py
+++ b/solution.py
@@ -135,7 +135,7 @@
 
 
 def fits(slabs, coefs, epoch_rows, coef_rows, columns, taps):
-    if slabs & (slabs - 1) or slabs < 4 or coefs % 2 or epoch_rows % (2 * LANES) or coef_rows % LANES:
+    if slabs & (slabs - 1) or slabs < 4 or coefs % 2 or coefs & (coefs - 1) or epoch_rows % (2 * LANES) or coef_rows % LANES:
         return False
     if coef_rows % slabs or taps != LANES or columns != LANES or columns != GROUP * slabs * coefs // 2:
         return False
@@ -144,13 +144,12 @@
     return owned >= 4 * LANES and rest >= 16 and LANES % rest == 0
 
 
-def flipped(index, bits, count):
-    result, weight = 0, 1
+def flips(index, count):
+    steps, weight = [], 1
     while weight < count:
-        bit = lax.rem(lax.div(index, weight), 2)
-        result = result + weight * (1 - bit if bits & weight else bit)
+        steps.append(weight * (1 - 2 * lax.rem(lax.div(index, weight), 2)))
         weight *= 2
-    return result
+    return [sum((step for at, step in enumerate(steps) if bits >> at & 1), index) for bits in range(count)]
 
 
 def pieces(values):
@@ -183,9 +182,9 @@
 
 def fused(plan, design, observed_in, gap_in, counts, taps_in, kaula_in, precond_in, solution_out, residual_out,
           observed, gap, taps, kaula, precond,
-          block, turned_block, edges, packed, loose, shown, seen, early, sums, received, total, sent, folded_in, sent_terms, terms_in,
+          block, turned_block, edges, packed, loose, shown, seen, seen_weight, early, sums, received, total, sent, folded_in, sent_terms, terms_in,
           whole, entering, weights, filtered, gathered, resid, direc, scal, solut, first_values,
-          own_sem, small_sem, edge_sem, block_send, block_recv, loose_recv, show_send, show_recv, early_send, early_recv,
+          own_sem, small_sem, edge_sem, block_send, block_recv, loose_recv, show_send, show_recv, weight_send, weight_recv, early_send, early_recv,
           early_relay_send, early_relay_recv, pair_send, pair_recv, fold_send, fold_recv, term_send, term_recv,
           whole_send, whole_recv, middle_send, middle_recv, gather_send, gather_recv, relay_send, relay_recv):
     slabs, chips, rows = plan.slabs, plan.chips, plan.epoch_rows
@@ -194,17 +193,14 @@
     across, core = lax.div(coef, 2), lax.rem(coef, 2)
     chip = slab * plan.across + across
     near_chip = lax.rem(chip, half_chips)
-    this_half = lax.div(chip, half_chips)
     partner = {"tm": slab, "coef": 2 * across + 1 - core}
 
-    def device(at):
-        return {"tm": lax.div(at, plan.across), "coef": 2 * lax.rem(at, plan.across) + core}
-
-    def other(step):
-        return lax.rem(chip + step, chips)
-
-    def near_other(step):
-        return lax.rem(near_chip + step, half_chips)
+    peers, sides = flips(slab, slabs), flips(across, plan.across)
+    targets = [
+        (peers[bits] * plan.across + sides[side], {"tm": peers[bits], "coef": coef + 2 * (sides[side] - across)})
+        for bits in reversed(range(slabs)) for side in reversed(range(plan.across)) if bits or side
+    ]
+    near_targets = targets[-(half_chips - 1):]
 
     def remote(src, dst, send, recv, target):
         return pltpu.make_async_remote_copy(
@@ -212,8 +208,8 @@
         )
 
     barrier = pltpu.get_barrier_semaphore()
-    for step in range(1, chips):
-        pl.semaphore_signal(barrier, inc=1, device_id=device(other(step)), device_id_type=MESH)
+    for _, target in targets:
+        pl.semaphore_signal(barrier, inc=1, device_id=target, device_id_type=MESH)
     pl.semaphore_signal(barrier, inc=1, device_id=partner, device_id_type=MESH)
 
     small = [
@@ -243,16 +239,20 @@
 
     for copy in small[:3]:
         copy.wait()
-    place = lax.broadcasted_iota(jnp.int32, (1, rows), 1)
-    present = jnp.concatenate([gap[at:at + 1, :] for at in range(rows // LANES)], 1)
-    weight_row = jnp.where((present == 1) & (place < counts[0]), 1.0, 0.0)
+    tall = rows // LANES
+    place = lax.broadcasted_iota(jnp.int32, (tall, LANES), 0) * LANES + lax.broadcasted_iota(jnp.int32, (tall, LANES), 1)
+    local_weight = jnp.where((gap[...] == 1) & (place < counts[0]), 1.0, 0.0)
+    seen_weight[slab] = local_weight
+    weight_row = jnp.concatenate([local_weight[at:at + 1] for at in range(tall)], 1)
     turned = observed[...].T * weight_row
-    shown[:, :GROUP, :] = turned.reshape(chips, GROUP, rows)
-    shown[:, GROUP:, :] = jnp.broadcast_to(weight_row[None], (chips, GROUP, rows))
+    shown[...] = turned.reshape(chips, GROUP, rows)
     seen[slab] = shown[2 * near_chip + core]
+    for turn in range(2):
+        for j in range(half_slabs):
+            folded_in[turn, j, chip] = jnp.zeros((GROUP, rows), jnp.bfloat16)
 
     def block_copy(bits, part):
-        peer = flipped(slab, bits, slabs)
+        peer = peers[bits]
         tile = plan.first_tile(peer) + 1
         if part == 0:
             src, dst = design.at[:, tile_columns(tile, plan.cut)], block.at[slab, :, pl.ds(0, plan.cut)]
@@ -266,7 +266,7 @@
         return remote(src, dst, block_send.at[part], loose_recv if part == 3 else block_recv.at[min(part, 1), slab], {"tm": peer, "coef": coef})
 
     def block_arrival(bits, part):
-        peer = flipped(slab, bits, slabs)
+        peer = peers[bits]
         low, size = ((0, plan.cut), (plan.cut, plan.mixed_at + LANES - plan.cut))[part]
         dst = block.at[peer, :, pl.ds(low, size)]
         return remote(dst, dst, block_send.at[part], block_recv.at[part, peer], {"tm": peer, "coef": coef})
@@ -275,14 +275,19 @@
         return remote(ref, ref, send, recv, partner)
 
     def show_copy(bits):
-        peer = flipped(slab, bits, slabs)
+        peer = peers[bits]
         src = shown.at[2 * lax.rem(peer * plan.across + across, half_chips) + core]
         return remote(src, seen.at[slab], show_send, show_recv, {"tm": peer, "coef": coef})
+
+    def weight_copy(bits):
+        src = seen_weight.at[slab]
+        return remote(src, src, weight_send, weight_recv, {"tm": peers[bits], "coef": coef})
 
     others = pl.ds(0, slabs - 1)
     pl.semaphore_wait(barrier, chips)
     for bits in range(1, slabs):
         show_copy(bits).start()
+        weight_copy(bits).start()
     for bits in range(1, half_slabs):
         block_copy(bits, 0).start()
         block_copy(bits, 1).start()
@@ -323,13 +328,13 @@
     blank = jnp.zeros((GROUP, LANES), jnp.float32)
 
     all_of(seen.at[others], show_send, show_recv).wait_recv()
-
-    def stack(ref, low):
-        return jnp.concatenate(
-            [ref[at, low:low + GROUP, j * LANES:(j + 1) * LANES] for at in range(slabs) for j in range(rows // LANES)], 0
-        )
-
-    weight = stack(seen, GROUP)
+    all_of(seen_weight.at[others], weight_send, weight_recv).wait_recv()
+
+    def repeated(at, j):
+        return jnp.broadcast_to(seen_weight[at, j:j + 1, :], (GROUP, LANES))
+
+    weight = jnp.concatenate([repeated(at, j) for at in range(slabs) for j in range(tall)], 0)
+    own_series = jnp.concatenate([seen[at, :, j * LANES:(j + 1) * LANES] for at in range(slabs) for j in range(tall)], 0)
 
     def weighted(values):
         entering = weight * values
@@ -347,8 +352,10 @@
         return which * (half_slabs + at) + (1 - which) * (half_slabs - 1 - at)
 
     for at in range(half_slabs):
-        for j, part in enumerate(nearer(seen[outward(at, core), GROUP:, :])):
-            weights[at * (rows // LANES) + j] = part
+        place_of = outward(at, core)
+        wide = jnp.concatenate([repeated(place_of, j) for j in range(tall)], 1)
+        for j, part in enumerate(nearer(wide)):
+            weights[at * tall + j] = part
     exact = lax.Precision.HIGHEST
     ends_block = product(lower, lower, NT, exact)
     same_block = ends_block + product(upper, upper, NT, exact)
@@ -357,13 +364,11 @@
     outside_block = jnp.where(core == 0, before_block, after_block)
     ends_block = jnp.where(core == 0, same_block, ends_block)
 
-    kept = weighted(stack(seen, 0)).astype(jnp.float32)
+    kept = weighted(own_series).astype(jnp.float32)
     for j in range(plan.blocks):
         early[core, near_chip, :, j * LANES:(j + 1) * LANES] = kept[j * GROUP:(j + 1) * GROUP].astype(jnp.bfloat16)
-    for step in range(1, half_chips):
-        to = near_other(step)
-        here = early.at[core, near_chip]
-        target = device(this_half * half_chips + to)
+    here = early.at[core, near_chip]
+    for _, target in near_targets:
         remote(here, here, early_send, early_recv, target).start()
     for bits in range(half_slabs, slabs):
         block_copy(bits, 1).start()
@@ -408,7 +413,7 @@
         turn_over(slab, span)
         resid[:, span] = product(series(slab), block[slab, :, span], NN)
         for bits in range(1, slabs):
-            peer = flipped(slab, bits, slabs)
+            peer = peers[bits]
             block_arrival(bits, part).wait_recv()
             if part:
                 unpack(peer, loose[peer])
@@ -428,30 +433,22 @@
         src = sums.at[turn, outward(j, 1 - core)]
         return remote(src, received.at[turn, j], pair_send.at[turn], pair_recv.at[turn, j], partner)
 
-    def fold_copy(turn, j, step):
-        to = other(step)
+    def fold_copy(turn, j, to, target):
         src, dst = sent.at[turn, j, to], folded_in.at[turn, j, chip]
-        return remote(src, dst, fold_send.at[turn], fold_recv.at[turn, j], device(to))
+        return remote(src, dst, fold_send.at[turn], fold_recv.at[turn, j], target)
 
     other_chips = pl.ds(0, chips - 1)
 
-    def term_copy(turn, step):
-        to = other(step)
+    def term_copy(turn, to, target):
         src, dst = sent_terms.at[turn, to], terms_in.at[turn, chip]
-        return remote(src, dst, term_send.at[turn], term_recv.at[turn], device(to))
-
-    def each_chip(action):
-        def body(at, carry):
-            action(half_chips + (1 - 2 * lax.rem(at, 2)) * lax.div(at + 1, 2))
-            return carry
-
-        lax.fori_loop(0, chips - 1, body, 0)
+        return remote(src, dst, term_send.at[turn], term_recv.at[turn], target)
 
     def filtered_sum(turn, low, terms, span, settle):
         scalars = in_lanes(terms, plan.columns)
         sent_terms[turn] = pieces(scalars).reshape(chips, GROUP, LANES).astype(jnp.bfloat16)
         terms_in[turn, chip] = sent_terms[turn, chip]
-        each_chip(lambda step: term_copy(turn, step).start())
+        for to, target in targets:
+            term_copy(turn, to, target).start()
 
         def partial(at):
             value = product(low, turned_block[at, span], NN)
@@ -468,25 +465,25 @@
             value = (value + received[turn, j]).reshape(chips, GROUP, rows)
             total[j] = value
             sent[turn, j] = value.astype(jnp.bfloat16)
-            each_chip(lambda step: fold_copy(turn, j, step).start())
+            for to, target in targets:
+                fold_copy(turn, j, to, target).start()
 
         def both(j, carry):
-            give(j + 1)
+            give(j + 2)
             keep(j)
             return carry
 
         give(0)
-        lax.fori_loop(0, half_slabs - 1, both, 0)
+        give(1)
+        lax.fori_loop(0, half_slabs - 2, both, 0)
+        keep(half_slabs - 2)
         keep(half_slabs - 1)
 
-        def added(ref, start):
-            def body(step, carry):
-                return carry + ref[other(step)].astype(jnp.float32)
-
-            return lax.fori_loop(1, chips, body, start, unroll=True)
+        def added(values):
+            return jnp.sum(values.astype(jnp.float32), 0)
 
         all_of(terms_in.at[turn, other_chips], term_send.at[turn], term_recv.at[turn]).wait_recv()
-        whole[turn, core] = added(terms_in.at[turn], terms_in[turn, chip].astype(jnp.float32))
+        whole[turn, core] = added(terms_in[turn])
         mine, theirs = whole.at[turn, core], whole.at[turn, 1 - core]
         remote(mine, mine, whole_send.at[turn], whole_recv.at[turn], partner).start()
         remote(theirs, theirs, whole_send.at[turn], whole_recv.at[turn], partner).wait_recv()
@@ -500,7 +497,7 @@
         entering[turn, half_blocks + 1] = blank
         for j in range(half_slabs):
             all_of(folded_in.at[turn, j, other_chips], fold_send.at[turn], fold_recv.at[turn, j]).wait_recv()
-            for at, value in enumerate(nearer(added(folded_in.at[turn, j], total[j, chip]))):
+            for at, value in enumerate(nearer(added(folded_in[turn, j]) + total[j, chip])):
                 at = j * per_slab + at
                 if ratio is not None:
                     value = value + ratio * first_values[0, at]
@@ -533,7 +530,8 @@
             if end == half_blocks:
                 parts.append(pieces(in_lanes([over(overlap)] + more, GROUP)))
             gathered[turn, group, core, chip, :, :len(parts) * LANES] = jnp.concatenate(parts, 1).astype(jnp.bfloat16)
-            each_chip(lambda step: gather_copy(turn, group, step).start())
+            for _, target in targets:
+                gather_copy(turn, group, target).start()
             group += 1
         for group in range(len(plan.groups)):
             everyone = gathered.at[turn, group, core, other_chips, :, pl.ds(0, extent(group))]
@@ -564,9 +562,9 @@
         src, dst = entering.at[turn, 1], entering.at[turn, 0]
         return remote(src if at else dst, dst, middle_send.at[turn], middle_recv.at[turn], partner)
 
-    def gather_copy(turn, group, step):
+    def gather_copy(turn, group, target):
         here = gathered.at[turn, group, core, chip, :, pl.ds(0, extent(group))]
-        return remote(here, here, gather_send.at[turn, group], gather_recv.at[turn, group], device(other(step)))
+        return remote(here, here, gather_send.at[turn, group], gather_recv.at[turn, group], target)
 
     def relay_copy(turn, group, which):
         here = gathered.at[turn, group, which, :, :, pl.ds(0, extent(group))]
@@ -624,6 +622,7 @@
         out[pl.ds(low, plan.rest), :] = end[:plan.rest]
 
     all_of(shown.at[others], show_send, show_recv).wait_send()
+    all_of(seen_weight.at[others], weight_send, weight_recv).wait_send()
     for part, (low, size) in enumerate(((0, plan.cut), (plan.cut, plan.mixed_at - plan.cut), (plan.mixed_at, LANES))):
         all_of(block.at[others, :, pl.ds(low, size)], block_send.at[part], loose_recv).wait_send()
     all_of(loose.at[others], block_send.at[3], loose_recv).wait_send()
@@ -674,8 +673,9 @@
             pltpu.VMEM((slabs, 2, epoch_rows, LANES), bf16),
             pltpu.VMEM((slabs, epoch_rows + plan.packed_rows, LANES), bf16),
             pltpu.VMEM((slabs, plan.packed_rows, LANES), bf16),
-            pltpu.VMEM((chips, 2 * GROUP, epoch_rows), f32),
-            pltpu.VMEM((slabs, 2 * GROUP, epoch_rows), f32),
+            pltpu.VMEM((chips, GROUP, epoch_rows), f32),
+            pltpu.VMEM((slabs, GROUP, epoch_rows), f32),
+            pltpu.VMEM((slabs, epoch_rows // LANES, LANES), f32),
             pltpu.VMEM((2, half_chips, GROUP, slabs * epoch_rows), bf16),
             pltpu.VMEM((2, slabs, columns, epoch_rows), f32),
             pltpu.VMEM((2, half_slabs, columns, epoch_rows), f32),
@@ -694,7 +694,7 @@
             pltpu.VMEM((columns, wide), f32),
             pltpu.VMEM((columns, wide), f32),
             pltpu.VMEM((2, plan.half_blocks, GROUP, LANES), f32),
-            sem(()), sem((5,)), sem(()), sem((4,)), sem((2, slabs)), sem(()), sem(()), sem(()),
+            sem(()), sem((5,)), sem(()), sem((4,)), sem((2, slabs)), *[sem(())] * 5,
             sem(()), sem(()), sem(()), sem(()),
             sem((2,)), sem((2, half_slabs)), sem((2,)), sem((2, half_slabs)), sem((2,)), sem((2,)), sem((2,)), sem((2,)),
             sem((2,)), sem((2,)), *[sem((2, len(plan.groups)))] * 4,

time: 193 us -> 190 us (0.984)
  Pallas kernels: 190 us -> 188 us
    pallas_call x1, Pallas kernels: 190 us -> 188 us  [fused_shards(): pl.pallas_call(functools.partial(fused, plan), out_shape=(shape, shape),...]
where the time goes in v5:
time: 190 us
  Pallas kernels  188 us (99%)
    pallas_call x1, Pallas kernels, fused_shards(): pl.pallas_call(functools.partial(fused, plan), out_shape=(shape, shape),...  188 us

profile of v5, /device:TPU:0, one launch (start us, length us, event | category | flops | bytes accessed | tf_op | source)
XLA Modules:
  0.0 190.1 jit_solution(3648899669926836765)
XLA Ops:
  1.3 187.5 %shard_map.86 = (f32[1792,128]{1,0:T(8,128)S(1)}, f32[1792,128]{1,0:T(8,128)S(1)}) custom-call(bf16[256,12544]{1,0:T(8,128)(2,1)} %design.1, f32[256,128]{1,0:T(8,128)} %observed_in.1, s32[2,128]{1,0:T(2,128)} %bitcast.6, s32[1]{0:T(128)S(6)} %copy.9.counts, f32[1,128]{1,0:T(1,128)} %bitcast.7, f32[98,128]{1,0:T(8,128)} %bitcast.4, f32[98,128]{1,0:T(8,128)} %bitcast.5), custom_call_target="tpu_custom_call" | custom-call | tf_op jit(solution)/shard_map/pallas_call | solution.py:660
  188.8 1.3 constant_dynamic-slice_fusion

commit v6 on v5

--- a/solution.py
+++ b/solution.py
@@ -128,6 +128,7 @@
         per_slab, half_slabs = epoch_rows // LANES, slabs // 2
         ends = [(upto + 1) * per_slab - 1 for upto in range(1, half_slabs - 1)] + [self.half_blocks]
         self.groups = list(zip([0] + ends[:-1], ends))
+        self.inner = (self.half_blocks - self.groups[-1][0], self.half_blocks + self.groups[-1][0])
         self.message = LANES * (1 + max(end - begin for begin, end in self.groups))
 
     def first_tile(self, owner):
@@ -183,7 +184,7 @@
 def fused(plan, design, observed_in, gap_in, counts, taps_in, kaula_in, precond_in, solution_out, residual_out,
           observed, gap, taps, kaula, precond,
           block, turned_block, edges, packed, loose, shown, seen, seen_weight, early, sums, received, total, sent, folded_in, sent_terms, terms_in,
-          whole, entering, weights, filtered, gathered, resid, direc, scal, solut, first_values,
+          whole, entering, weights, filtered, gathered, resid, direc, scal, solut, image, first_values,
           own_sem, small_sem, edge_sem, block_send, block_recv, loose_recv, show_send, show_recv, weight_send, weight_recv, early_send, early_recv,
           early_relay_send, early_relay_recv, pair_send, pair_recv, fold_send, fold_recv, term_send, term_recv,
           whole_send, whole_recv, middle_send, middle_recv, gather_send, gather_recv, relay_send, relay_recv):
@@ -403,6 +404,7 @@
 
     own.wait()
     spans = (slice(0, plan.cut), slice(plan.cut, plan.width))
+    part_terms = []
 
     def turn_over(at, span):
         turned_block[at, span] = block[at, :, span].T
@@ -428,6 +430,8 @@
                 return carry
 
             lax.fori_loop(0, slabs, body, 0)
+        ridged = ridge_row[:, span] * direc[:, span]
+        part_terms.append((over(resid[:, span] * direc[:, span]), over(ridged * direc[:, span])))
 
     def pair_copy(turn, j):
         src = sums.at[turn, outward(j, 1 - core)]
@@ -443,13 +447,22 @@
         src, dst = sent_terms.at[turn, to], terms_in.at[turn, chip]
         return remote(src, dst, term_send.at[turn], term_recv.at[turn], target)
 
+    chunks = [slice(low, min(low + 2 * LANES, plan.width)) for low in range(0, plan.width, 2 * LANES)]
+
+    def transposed(span, blocks):
+        begin, end = blocks
+        parts, at = [], begin
+        while at < end:
+            upto = min(end, (at // tall + 1) * tall)
+            parts.append(block[at // tall, at % tall * LANES:(upto - at // tall * tall) * LANES, span])
+            at = upto
+        return product(filtered[:, begin * LANES:end * LANES], jnp.concatenate(parts, 0), NN)
+
+    def transposed_rest(span):
+        begin, end = plan.inner
+        return image[:, span] + transposed(span, (0, begin)) + transposed(span, (end, plan.blocks))
+
     def filtered_sum(turn, low, terms, span, settle):
-        scalars = in_lanes(terms, plan.columns)
-        sent_terms[turn] = pieces(scalars).reshape(chips, GROUP, LANES).astype(jnp.bfloat16)
-        terms_in[turn, chip] = sent_terms[turn, chip]
-        for to, target in targets:
-            term_copy(turn, to, target).start()
-
         def partial(at):
             value = product(low, turned_block[at, span], NN)
             return value + sums[turn, at] if turn == 0 else value
@@ -475,6 +488,11 @@
 
         give(0)
         give(1)
+        scalars = in_lanes(terms, plan.columns)
+        sent_terms[turn] = pieces(scalars).reshape(chips, GROUP, LANES).astype(jnp.bfloat16)
+        terms_in[turn, chip] = sent_terms[turn, chip]
+        for to, target in targets:
+            term_copy(turn, to, target).start()
         lax.fori_loop(0, half_slabs - 2, both, 0)
         keep(half_slabs - 2)
         keep(half_slabs - 1)
@@ -533,11 +551,8 @@
             for _, target in targets:
                 gather_copy(turn, group, target).start()
             group += 1
-        for group in range(len(plan.groups)):
-            everyone = gathered.at[turn, group, core, other_chips, :, pl.ds(0, extent(group))]
-            all_of(everyone, gather_send.at[turn, group], gather_recv.at[turn, group]).wait_recv()
-            relay_copy(turn, group, core).start()
-        for group, (begin, end) in enumerate(plan.groups):
+        def unfold(group):
+            begin, end = plan.groups[group]
             relay_copy(turn, group, 1 - core).wait_recv()
             for half in range(2):
                 for at in range(begin, end):
@@ -545,6 +560,16 @@
                     part = part.astype(jnp.float32).reshape(plan.columns, LANES).astype(jnp.bfloat16)
                     low = (half_blocks + at if half else half_blocks - 1 - at) * LANES
                     filtered[:, low:low + LANES] = part
+
+        for group in range(len(plan.groups)):
+            everyone = gathered.at[turn, group, core, other_chips, :, pl.ds(0, extent(group))]
+            all_of(everyone, gather_send.at[turn, group], gather_recv.at[turn, group]).wait_recv()
+            relay_copy(turn, group, core).start()
+        for group in range(len(plan.groups) - 1):
+            unfold(group)
+        for span in chunks:
+            image[:, span] = transposed(span, plan.inner)
+        unfold(len(plan.groups) - 1)
         last = len(plan.groups) - 1
         span = slice(extent(last) - LANES, extent(last))
         first_terms, second_terms = [
@@ -570,20 +595,13 @@
         here = gathered.at[turn, group, which, :, :, pl.ds(0, extent(group))]
         return remote(here, here, relay_send.at[turn, group], relay_recv.at[turn, group], partner)
 
-    chunks = [slice(low, min(low + 2 * LANES, plan.width)) for low in range(0, plan.width, 2 * LANES)]
-
-    def transposed(span):
-        part = block[:, :, span]
-        return product(filtered[...], part.reshape(slabs * rows, part.shape[2]), NN)
-
-    ridged = ridge_row * direc[...]
-    terms = [over(resid[...] * direc[...]), over(ridged * direc[...])]
+    terms = [left + right for left, right in zip(*part_terms)]
     low = direc[:, spans[1]].astype(jnp.bfloat16)
     (norm, ridge), _, step_col, _ = filtered_sum(0, low, terms, spans[1], lambda sums_of: (None, list(sums_of)))
     terms = [0.0, 0.0, 0.0]
     for span in chunks:
         along, ridge_part = direc[:, span], ridge_row[:, span]
-        left = resid[:, span] - step_col * (transposed(span) + ridge_part * along)
+        left = resid[:, span] - step_col * (transposed_rest(span) + ridge_part * along)
         ahead = scale_row[:, span] * left
         resid[:, span] = left
         solut[:, span] = step_col * along
@@ -607,7 +625,7 @@
     for span in chunks:
         along = scal[:, span] + ratio_col * direc[:, span]
         ahead = solut[:, span] + step_col * along
-        left = resid[:, span] - step_col * (transposed(span) + ridge_row[:, span] * along)
+        left = resid[:, span] - step_col * (transposed_rest(span) + ridge_row[:, span] * along)
         for low in range(0, span.stop - span.start, LANES):
             held[(span.start + low) // LANES] = (ahead[:, low:low + LANES].T, left[:, low:low + LANES].T)
         for tile in [tile for tile in held if tile < plan.full]:
@@ -693,6 +711,7 @@
             pltpu.VMEM((columns, wide), f32),
             pltpu.VMEM((columns, wide), f32),
             pltpu.VMEM((columns, wide), f32),
+            pltpu.VMEM((columns, wide), f32),
             pltpu.VMEM((2, plan.half_blocks, GROUP, LANES), f32),
             sem(()), sem((5,)), sem(()), sem((4,)), sem((2, slabs)), *[sem(())] * 5,
             sem(()), sem(()), sem(()), sem(()),

time: 190 us -> 189 us (level)
  Pallas kernels: 188 us -> 186 us
where the time goes in v6:
time: 189 us
  Pallas kernels  186 us (98%)
    pallas_call x1, Pallas kernels, fused_shards(): pl.pallas_call(functools.partial(fused, plan), out_shape=(shape, shape),...  186 us

profile of v6, /device:TPU:0, one launch (start us, length us, event | category | flops | bytes accessed | tf_op | source)
XLA Modules:
  0.0 188.7 jit_solution(2022167563067860474)
XLA Ops:
  1.3 186.2 %shard_map.86 = (f32[1792,128]{1,0:T(8,128)S(1)}, f32[1792,128]{1,0:T(8,128)S(1)}) custom-call(bf16[256,12544]{1,0:T(8,128)(2,1)} %design.1, f32[256,128]{1,0:T(8,128)} %observed_in.1, s32[2,128]{1,0:T(2,128)} %bitcast.6, s32[1]{0:T(128)S(6)} %copy.9.counts, f32[1,128]{1,0:T(1,128)} %bitcast.7, f32[98,128]{1,0:T(8,128)} %bitcast.4, f32[98,128]{1,0:T(8,128)} %bitcast.5), custom_call_target="tpu_custom_call" | custom-call | tf_op jit(solution)/shard_map/pallas_call | solution.py:678
  187.5 1.3 constant_dynamic-slice_fusion

commit v7 on v6

--- a/solution.py
+++ b/solution.py
@@ -105,6 +105,7 @@
 
 LANES = 128
 GROUP = 8
+PAIRED = 2 * GROUP
 MESH = pl.DeviceIdType.MESH
 NN = ((1,), (0,))
 NT = ((1,), (1,))
@@ -184,10 +185,10 @@
 def fused(plan, design, observed_in, gap_in, counts, taps_in, kaula_in, precond_in, solution_out, residual_out,
           observed, gap, taps, kaula, precond,
           block, turned_block, edges, packed, loose, shown, seen, seen_weight, early, sums, received, total, sent, folded_in, sent_terms, terms_in,
-          whole, entering, weights, filtered, gathered, resid, direc, scal, solut, image, first_values,
+          whole, whole_parts, crossed, entering, weights, filtered, gathered, resid, direc, scal, solut, image, first_values,
           own_sem, small_sem, edge_sem, block_send, block_recv, loose_recv, show_send, show_recv, weight_send, weight_recv, early_send, early_recv,
           early_relay_send, early_relay_recv, pair_send, pair_recv, fold_send, fold_recv, term_send, term_recv,
-          whole_send, whole_recv, middle_send, middle_recv, gather_send, gather_recv, relay_send, relay_recv):
+          whole_send, whole_recv, cross_send, cross_recv, middle_send, middle_recv, gather_send, gather_recv, relay_send, relay_recv):
     slabs, chips, rows = plan.slabs, plan.chips, plan.epoch_rows
     half_slabs, half_chips, half_blocks = slabs // 2, chips // 2, plan.half_blocks
     slab, coef = lax.axis_index("tm"), lax.axis_index("coef")
@@ -201,7 +202,12 @@
         (peers[bits] * plan.across + sides[side], {"tm": peers[bits], "coef": coef + 2 * (sides[side] - across)})
         for bits in reversed(range(slabs)) for side in reversed(range(plan.across)) if bits or side
     ]
-    near_targets = targets[-(half_chips - 1):]
+    near_targets = [
+        (at - lax.div(slab, half_slabs) * half_chips, target) for at, target in targets[-(half_chips - 1):]
+    ]
+    this_half = lax.div(slab, half_slabs)
+    mirror = {"tm": peers[half_slabs], "coef": coef}
+    across_mirror = {"tm": peers[half_slabs], "coef": 2 * across + 1 - core}
 
     def remote(src, dst, send, recv, target):
         return pltpu.make_async_remote_copy(
@@ -211,7 +217,8 @@
     barrier = pltpu.get_barrier_semaphore()
     for _, target in targets:
         pl.semaphore_signal(barrier, inc=1, device_id=target, device_id_type=MESH)
-    pl.semaphore_signal(barrier, inc=1, device_id=partner, device_id_type=MESH)
+    for target in (partner, across_mirror):
+        pl.semaphore_signal(barrier, inc=1, device_id=target, device_id_type=MESH)
 
     small = [
         pltpu.make_async_copy(src, dst, small_sem.at[at])
@@ -250,7 +257,7 @@
     seen[slab] = shown[2 * near_chip + core]
     for turn in range(2):
         for j in range(half_slabs):
-            folded_in[turn, j, chip] = jnp.zeros((GROUP, rows), jnp.bfloat16)
+            folded_in[turn, j, near_chip] = jnp.zeros((PAIRED, rows), jnp.bfloat16)
 
     def block_copy(bits, part):
         peer = peers[bits]
@@ -285,7 +292,7 @@
         return remote(src, src, weight_send, weight_recv, {"tm": peers[bits], "coef": coef})
 
     others = pl.ds(0, slabs - 1)
-    pl.semaphore_wait(barrier, chips)
+    pl.semaphore_wait(barrier, chips + 1)
     for bits in range(1, slabs):
         show_copy(bits).start()
         weight_copy(bits).start()
@@ -356,7 +363,7 @@
         place_of = outward(at, core)
         wide = jnp.concatenate([repeated(place_of, j) for j in range(tall)], 1)
         for j, part in enumerate(nearer(wide)):
-            weights[at * tall + j] = part
+            weights[at * tall + j] = jnp.concatenate([part, part], 0)
     exact = lax.Precision.HIGHEST
     ends_block = product(lower, lower, NT, exact)
     same_block = ends_block + product(upper, upper, NT, exact)
@@ -438,13 +445,20 @@
         return remote(src, received.at[turn, j], pair_send.at[turn], pair_recv.at[turn, j], partner)
 
     def fold_copy(turn, j, to, target):
-        src, dst = sent.at[turn, j, to], folded_in.at[turn, j, chip]
+        src, dst = sent.at[turn, j, to], folded_in.at[turn, j, near_chip]
         return remote(src, dst, fold_send.at[turn], fold_recv.at[turn, j], target)
 
-    other_chips = pl.ds(0, chips - 1)
+    def cross_copy(turn, j):
+        here = crossed.at[turn, j, this_half]
+        return remote(here, here, cross_send.at[turn], cross_recv.at[turn, j], mirror)
+
+    def whole_copy(turn, target):
+        here = whole.at[turn, this_half, core]
+        return remote(here, here, whole_send.at[turn], whole_recv.at[turn], target)
+
 
     def term_copy(turn, to, target):
-        src, dst = sent_terms.at[turn, to], terms_in.at[turn, chip]
+        src, dst = sent_terms.at[turn, to], terms_in.at[turn, near_chip]
         return remote(src, dst, term_send.at[turn], term_recv.at[turn], target)
 
     chunks = [slice(low, min(low + 2 * LANES, plan.width)) for low in range(0, plan.width, 2 * LANES)]
@@ -475,10 +489,10 @@
         def keep(j):
             value = partial(outward(j, core))
             pair_copy(turn, j).wait_recv()
-            value = (value + received[turn, j]).reshape(chips, GROUP, rows)
+            value = (value + received[turn, j]).reshape(half_chips, PAIRED, rows)
             total[j] = value
             sent[turn, j] = value.astype(jnp.bfloat16)
-            for to, target in targets:
+            for to, target in near_targets:
                 fold_copy(turn, j, to, target).start()
 
         def both(j, carry):
@@ -489,9 +503,9 @@
         give(0)
         give(1)
         scalars = in_lanes(terms, plan.columns)
-        sent_terms[turn] = pieces(scalars).reshape(chips, GROUP, LANES).astype(jnp.bfloat16)
-        terms_in[turn, chip] = sent_terms[turn, chip]
-        for to, target in targets:
+        sent_terms[turn] = pieces(scalars).reshape(half_chips, PAIRED, LANES).astype(jnp.bfloat16)
+        terms_in[turn, near_chip] = sent_terms[turn, near_chip]
+        for to, target in near_targets:
             term_copy(turn, to, target).start()
         lax.fori_loop(0, half_slabs - 2, both, 0)
         keep(half_slabs - 2)
@@ -500,22 +514,29 @@
         def added(values):
             return jnp.sum(values.astype(jnp.float32), 0)
 
-        all_of(terms_in.at[turn, other_chips], term_send.at[turn], term_recv.at[turn]).wait_recv()
-        whole[turn, core] = added(terms_in[turn])
-        mine, theirs = whole.at[turn, core], whole.at[turn, 1 - core]
-        remote(mine, mine, whole_send.at[turn], whole_recv.at[turn], partner).start()
-        remote(theirs, theirs, whole_send.at[turn], whole_recv.at[turn], partner).wait_recv()
-        scalars = whole[turn, 0] + whole[turn, 1]
-        scalars = [joined(scalars, at) for at in range(len(terms))]
+        all_of(terms_in.at[turn, near_others], term_send.at[turn], term_recv.at[turn]).wait_recv()
+        half_terms = added(terms_in[turn])
+        half_terms = half_terms + pltpu.roll(half_terms, LANES - 8, 1) + pltpu.roll(half_terms, LANES - 16, 1)
+        whole[turn, this_half, core] = half_terms
+        for target in (mirror, across_mirror, partner):
+            whole_copy(turn, target).start()
+        for j in range(half_slabs):
+            all_of(folded_in.at[turn, j, near_others], fold_send.at[turn], fold_recv.at[turn, j]).wait_recv()
+            crossed[turn, j, this_half] = added(folded_in[turn, j]) + total[j, near_chip]
+            cross_copy(turn, j).start()
+        all_of(whole_parts.at[pl.ds(0, 3)], whole_send.at[turn], whole_recv.at[turn]).wait_recv()
+        scalars = (whole[turn, 0, 0] + whole[turn, 0, 1]) + (whole[turn, 1, 0] + whole[turn, 1, 1])
+        scalars = [scalars[:, at:at + 1] for at in range(len(terms))]
         ratio, more = settle(scalars)
 
         per_slab = rows // LANES
-        overlap = jnp.zeros((GROUP, LANES), jnp.float32)
+        overlap = jnp.zeros((PAIRED, LANES), jnp.float32)
         group = 0
-        entering[turn, half_blocks + 1] = blank
+        entering[turn, half_blocks + 1] = jnp.zeros((PAIRED, LANES), jnp.float32)
         for j in range(half_slabs):
-            all_of(folded_in.at[turn, j, other_chips], fold_send.at[turn], fold_recv.at[turn, j]).wait_recv()
-            for at, value in enumerate(nearer(added(folded_in[turn, j]) + total[j, chip])):
+            theirs = crossed.at[turn, j, 1 - this_half]
+            remote(theirs, theirs, cross_send.at[turn], cross_recv.at[turn, j], mirror).wait_recv()
+            for at, value in enumerate(nearer(crossed[turn, j, 0] + crossed[turn, j, 1])):
                 at = j * per_slab + at
                 if ratio is not None:
                     value = value + ratio * first_values[0, at]
@@ -530,25 +551,25 @@
             count = end - begin
 
             def rows_of(ref):
-                return ref.reshape(count * GROUP, LANES)
+                return ref.reshape(count * PAIRED, LANES)
 
             here = rows_of(entering[turn, begin + 1:end + 1])
             outer = product(rows_of(entering[turn, begin:end]), inside_block, NN, exact)
             outer = outer + product(rows_of(entering[turn, begin + 2:end + 2]), outside_block, NN, exact)
             if end == half_blocks:
                 kept = jnp.concatenate([
-                    product(here[:-GROUP], same_block, NN, exact), product(here[-GROUP:], ends_block, NN, exact)
+                    product(here[:-PAIRED], same_block, NN, exact), product(here[-PAIRED:], ends_block, NN, exact)
                 ], 0)
             else:
                 kept = product(here, same_block, NN, exact)
             kept = (rows_of(weights[begin:end]) * (outer + kept)).astype(jnp.bfloat16).astype(jnp.float32)
             with_values = rows_of(first_values[turn, begin:end]) * kept
-            overlap = overlap + jnp.sum(with_values.reshape(count, GROUP, LANES), 0)
-            parts = [kept[at * GROUP:(at + 1) * GROUP] for at in range(count)]
+            overlap = overlap + jnp.sum(with_values.reshape(count, PAIRED, LANES), 0)
+            parts = [kept[at * PAIRED:(at + 1) * PAIRED] for at in range(count)]
             if end == half_blocks:
-                parts.append(pieces(in_lanes([over(overlap)] + more, GROUP)))
-            gathered[turn, group, core, chip, :, :len(parts) * LANES] = jnp.concatenate(parts, 1).astype(jnp.bfloat16)
-            for _, target in targets:
+                parts.append(pieces(in_lanes([over(overlap)] + more, PAIRED)))
+            gathered[turn, group, core, near_chip, :, :len(parts) * LANES] = jnp.concatenate(parts, 1).astype(jnp.bfloat16)
+            for _, target in near_targets:
                 gather_copy(turn, group, target).start()
             group += 1
         def unfold(group):
@@ -557,12 +578,12 @@
             for half in range(2):
                 for at in range(begin, end):
                     part = gathered[turn, group, half, :, :, (at - begin) * LANES:(at - begin + 1) * LANES]
-                    part = part.astype(jnp.float32).reshape(plan.columns, LANES).astype(jnp.bfloat16)
+                    part = part.reshape(plan.columns, LANES)
                     low = (half_blocks + at if half else half_blocks - 1 - at) * LANES
                     filtered[:, low:low + LANES] = part
 
         for group in range(len(plan.groups)):
-            everyone = gathered.at[turn, group, core, other_chips, :, pl.ds(0, extent(group))]
+            everyone = gathered.at[turn, group, core, near_others, :, pl.ds(0, extent(group))]
             all_of(everyone, gather_send.at[turn, group], gather_recv.at[turn, group]).wait_recv()
             relay_copy(turn, group, core).start()
         for group in range(len(plan.groups) - 1):
@@ -588,7 +609,7 @@
         return remote(src if at else dst, dst, middle_send.at[turn], middle_recv.at[turn], partner)
 
     def gather_copy(turn, group, target):
-        here = gathered.at[turn, group, core, chip, :, pl.ds(0, extent(group))]
+        here = gathered.at[turn, group, core, near_chip, :, pl.ds(0, extent(group))]
         return remote(here, here, gather_send.at[turn, group], gather_recv.at[turn, group], target)
 
     def relay_copy(turn, group, which):
@@ -648,12 +669,13 @@
     all_of(early.at[core], early_relay_send, early_relay_recv).wait_send()
     for turn in range(2):
         all_of(received.at[turn], pair_send.at[turn], pair_recv.at[turn, 0]).wait_send()
-        all_of(sent.at[turn, :, other_chips], fold_send.at[turn], fold_recv.at[turn, 0]).wait_send()
-        all_of(sent_terms.at[turn, other_chips], term_send.at[turn], term_recv.at[turn]).wait_send()
-        all_of(whole.at[turn, core], whole_send.at[turn], whole_recv.at[turn]).wait_send()
+        all_of(sent.at[turn, :, near_others], fold_send.at[turn], fold_recv.at[turn, 0]).wait_send()
+        all_of(sent_terms.at[turn, near_others], term_send.at[turn], term_recv.at[turn]).wait_send()
+        all_of(whole_parts.at[pl.ds(0, 3)], whole_send.at[turn], whole_recv.at[turn]).wait_send()
+        all_of(crossed.at[turn, :, 0], cross_send.at[turn], cross_recv.at[turn, 0]).wait_send()
         middle_copy(turn, 1).wait_send()
         for group in range(len(plan.groups)):
-            everyone = gathered.at[turn, group, core, other_chips, :, pl.ds(0, extent(group))]
+            everyone = gathered.at[turn, group, core, near_others, :, pl.ds(0, extent(group))]
             all_of(everyone, gather_send.at[turn, group], gather_recv.at[turn, group]).wait_send()
             relay_copy(turn, group, core).wait_send()
 
@@ -697,25 +719,27 @@
             pltpu.VMEM((2, half_chips, GROUP, slabs * epoch_rows), bf16),
             pltpu.VMEM((2, slabs, columns, epoch_rows), f32),
             pltpu.VMEM((2, half_slabs, columns, epoch_rows), f32),
-            pltpu.VMEM((half_slabs, chips, GROUP, epoch_rows), f32),
-            pltpu.VMEM((2, half_slabs, chips, GROUP, epoch_rows), bf16),
-            pltpu.VMEM((2, half_slabs, chips, GROUP, epoch_rows), bf16),
-            pltpu.VMEM((2, chips, GROUP, LANES), bf16),
-            pltpu.VMEM((2, chips, GROUP, LANES), bf16),
-            pltpu.VMEM((2, 2, GROUP, LANES), f32),
-            pltpu.VMEM((2, plan.half_blocks + 2, GROUP, LANES), f32),
-            pltpu.VMEM((plan.half_blocks, GROUP, LANES), f32),
+            pltpu.VMEM((half_slabs, half_chips, PAIRED, epoch_rows), f32),
+            pltpu.VMEM((2, half_slabs, half_chips, PAIRED, epoch_rows), bf16),
+            pltpu.VMEM((2, half_slabs, half_chips, PAIRED, epoch_rows), bf16),
+            pltpu.VMEM((2, half_chips, PAIRED, LANES), bf16),
+            pltpu.VMEM((2, half_chips, PAIRED, LANES), bf16),
+            pltpu.VMEM((2, 2, 2, PAIRED, LANES), f32),
+            pltpu.VMEM((4, PAIRED, LANES), f32),
+            pltpu.VMEM((2, half_slabs, 2, PAIRED, epoch_rows), f32),
+            pltpu.VMEM((2, plan.half_blocks + 2, PAIRED, LANES), f32),
+            pltpu.VMEM((plan.half_blocks, PAIRED, LANES), f32),
             pltpu.VMEM((columns, slabs * epoch_rows), bf16),
-            pltpu.VMEM((2, len(plan.groups), 2, chips, GROUP, message), bf16),
+            pltpu.VMEM((2, len(plan.groups), 2, half_chips, PAIRED, message), bf16),
             pltpu.VMEM((columns, wide), f32),
             pltpu.VMEM((columns, wide), f32),
             pltpu.VMEM((columns, wide), f32),
             pltpu.VMEM((columns, wide), f32),
             pltpu.VMEM((columns, wide), f32),
-            pltpu.VMEM((2, plan.half_blocks, GROUP, LANES), f32),
+            pltpu.VMEM((2, plan.half_blocks, PAIRED, LANES), f32),
             sem(()), sem((5,)), sem(()), sem((4,)), sem((2, slabs)), *[sem(())] * 5,
             sem(()), sem(()), sem(()), sem(()),
-            sem((2,)), sem((2, half_slabs)), sem((2,)), sem((2, half_slabs)), sem((2,)), sem((2,)), sem((2,)), sem((2,)),
+            sem((2,)), sem((2, half_slabs)), sem((2,)), sem((2, half_slabs)), sem((2,)), sem((2,)), sem((2,)), sem((2,)), sem((2,)), sem((2, half_slabs)),
             sem((2,)), sem((2,)), *[sem((2, len(plan.groups)))] * 4,
         ],
         compiler_params=pltpu.CompilerParams(

time: 189 us -> 185 us (0.979)
  Pallas kernels: 186 us -> 183 us
    pallas_call x1, Pallas kernels: 186 us -> 183 us  [fused_shards(): pl.pallas_call(functools.partial(fused, plan), out_shape=(shape, shape),...]
where the time goes in v7:
time: 185 us
  Pallas kernels  183 us (99%)
    pallas_call x1, Pallas kernels, fused_shards(): pl.pallas_call(functools.partial(fused, plan), out_shape=(shape, shape),...  183 us

profile of v7, /device:TPU:0, one launch (start us, length us, event | category | flops | bytes accessed | tf_op | source)
XLA Modules:
  0.0 185.3 jit_solution(795773222356098173)
XLA Ops:
  1.3 182.7 %shard_map.86 = (f32[1792,128]{1,0:T(8,128)S(1)}, f32[1792,128]{1,0:T(8,128)S(1)}) custom-call(bf16[256,12544]{1,0:T(8,128)(2,1)} %design.1, f32[256,128]{1,0:T(8,128)} %observed_in.1, s32[2,128]{1,0:T(2,128)} %bitcast.6, s32[1]{0:T(128)S(6)} %copy.9.counts, f32[1,128]{1,0:T(1,128)} %bitcast.7, f32[98,128]{1,0:T(8,128)} %bitcast.4, f32[98,128]{1,0:T(8,128)} %bitcast.5), custom_call_target="tpu_custom_call" | custom-call | tf_op jit(solution)/shard_map/pallas_call | solution.py:700
  184.0 1.3 constant_dynamic-slice_fusion

commit v8 on v7

--- a/solution.py
+++ b/solution.py
@@ -208,6 +208,11 @@
     this_half = lax.div(slab, half_slabs)
     mirror = {"tm": peers[half_slabs], "coef": coef}
     across_mirror = {"tm": peers[half_slabs], "coef": 2 * across + 1 - core}
+    met = [
+        {"tm": peers[bits], "coef": coef + 2 * (sides[side] - across)}
+        for bits in range(slabs) for side in range(plan.across)
+        if (bits or side) and (bits < half_slabs or not side)
+    ] + [partner, across_mirror]
 
     def remote(src, dst, send, recv, target):
         return pltpu.make_async_remote_copy(
@@ -215,9 +220,7 @@
         )
 
     barrier = pltpu.get_barrier_semaphore()
-    for _, target in targets:
-        pl.semaphore_signal(barrier, inc=1, device_id=target, device_id_type=MESH)
-    for target in (partner, across_mirror):
+    for target in met:
         pl.semaphore_signal(barrier, inc=1, device_id=target, device_id_type=MESH)
 
     small = [
@@ -292,7 +295,7 @@
         return remote(src, src, weight_send, weight_recv, {"tm": peers[bits], "coef": coef})
 
     others = pl.ds(0, slabs - 1)
-    pl.semaphore_wait(barrier, chips + 1)
+    pl.semaphore_wait(barrier, len(met))
     for bits in range(1, slabs):
         show_copy(bits).start()
         weight_copy(bits).start()
@@ -481,13 +484,11 @@
             value = product(low, turned_block[at, span], NN)
             return value + sums[turn, at] if turn == 0 else value
 
-        def give(j):
-            at = outward(j, 1 - core)
-            sums[turn, at] = partial(at)
+        def give(j, value):
+            sums[turn, outward(j, 1 - core)] = value
             pair_copy(turn, j).start()
 
-        def keep(j):
-            value = partial(outward(j, core))
+        def keep(j, value):
             pair_copy(turn, j).wait_recv()
             value = (value + received[turn, j]).reshape(half_chips, PAIRED, rows)
             total[j] = value
@@ -495,21 +496,30 @@
             for to, target in near_targets:
                 fold_copy(turn, j, to, target).start()
 
+        def theirs_at(j):
+            return partial(outward(j, 1 - core))
+
+        def ours_at(j):
+            return partial(outward(j, core))
+
         def both(j, carry):
-            give(j + 2)
-            keep(j)
+            theirs, ours = theirs_at(j + 2), ours_at(j)
+            give(j + 2, theirs)
+            keep(j, ours)
             return carry
 
-        give(0)
-        give(1)
+        first_value, second_value = theirs_at(0), theirs_at(1)
+        give(0, first_value)
+        give(1, second_value)
         scalars = in_lanes(terms, plan.columns)
         sent_terms[turn] = pieces(scalars).reshape(half_chips, PAIRED, LANES).astype(jnp.bfloat16)
         terms_in[turn, near_chip] = sent_terms[turn, near_chip]
         for to, target in near_targets:
             term_copy(turn, to, target).start()
         lax.fori_loop(0, half_slabs - 2, both, 0)
-        keep(half_slabs - 2)
-        keep(half_slabs - 1)
+        first_value, second_value = ours_at(half_slabs - 2), ours_at(half_slabs - 1)
+        keep(half_slabs - 2, first_value)
+        keep(half_slabs - 1, second_value)
 
         def added(values):
             return jnp.sum(values.astype(jnp.float32), 0)
@@ -524,10 +534,15 @@
             all_of(folded_in.at[turn, j, near_others], fold_send.at[turn], fold_recv.at[turn, j]).wait_recv()
             crossed[turn, j, this_half] = added(folded_in[turn, j]) + total[j, near_chip]
             cross_copy(turn, j).start()
-        all_of(whole_parts.at[pl.ds(0, 3)], whole_send.at[turn], whole_recv.at[turn]).wait_recv()
-        scalars = (whole[turn, 0, 0] + whole[turn, 0, 1]) + (whole[turn, 1, 0] + whole[turn, 1, 1])
-        scalars = [scalars[:, at:at + 1] for at in range(len(terms))]
-        ratio, more = settle(scalars)
+        def settled():
+            all_of(whole_parts.at[pl.ds(0, 3)], whole_send.at[turn], whole_recv.at[turn]).wait_recv()
+            scalars = (whole[turn, 0, 0] + whole[turn, 0, 1]) + (whole[turn, 1, 0] + whole[turn, 1, 1])
+            scalars = [scalars[:, at:at + 1] for at in range(len(terms))]
+            return scalars, *settle(scalars)
+
+        ratio = None
+        if turn:
+            scalars, ratio, more = settled()
 
         per_slab = rows // LANES
         overlap = jnp.zeros((PAIRED, LANES), jnp.float32)
@@ -567,6 +582,8 @@
             overlap = overlap + jnp.sum(with_values.reshape(count, PAIRED, LANES), 0)
             parts = [kept[at * PAIRED:(at + 1) * PAIRED] for at in range(count)]
             if end == half_blocks:
+                if not turn:
+                    scalars, _, more = settled()
                 parts.append(pieces(in_lanes([over(overlap)] + more, PAIRED)))
             gathered[turn, group, core, near_chip, :, :len(parts) * LANES] = jnp.concatenate(parts, 1).astype(jnp.bfloat16)
             for _, target in near_targets:
@@ -582,15 +599,22 @@
                     low = (half_blocks + at if half else half_blocks - 1 - at) * LANES
                     filtered[:, low:low + LANES] = part
 
-        for group in range(len(plan.groups)):
+        final = len(plan.groups) - 1
+        for group in range(final + 1):
             everyone = gathered.at[turn, group, core, near_others, :, pl.ds(0, extent(group))]
             all_of(everyone, gather_send.at[turn, group], gather_recv.at[turn, group]).wait_recv()
             relay_copy(turn, group, core).start()
-        for group in range(len(plan.groups) - 1):
-            unfold(group)
-        for span in chunks:
-            image[:, span] = transposed(span, plan.inner)
-        unfold(len(plan.groups) - 1)
+            if group < 1 or group > final:
+                continue
+            unfold(group - 1)
+            begin, end = plan.groups[group - 1]
+            low, high = half_blocks - end, half_blocks + end
+            ranges = [(low, half_blocks - begin), (half_blocks + begin, high)] if begin else [(low, high)]
+            for span in chunks:
+                for at, blocks in enumerate(ranges):
+                    value = transposed(span, blocks)
+                    image[:, span] = image[:, span] + value if group > 1 or at else value
+        unfold(final)
         last = len(plan.groups) - 1
         span = slice(extent(last) - LANES, extent(last))
         first_terms, second_terms = [

time: 185 us -> 185 us (level)
  no operation moved by 1% of the time
where the time goes in v8:
time: 185 us
  Pallas kernels  182 us (98%)
    pallas_call x1, Pallas kernels, fused_shards(): pl.pallas_call(functools.partial(fused, plan), out_shape=(shape, shape),...  182 us

profile of v8, /device:TPU:0, one launch (start us, length us, event | category | flops | bytes accessed | tf_op | source)
XLA Modules:
  0.0 184.9 jit_solution(11441973783606977986)
XLA Ops:
  1.3 182.3 %shard_map.86 = (f32[1792,128]{1,0:T(8,128)S(1)}, f32[1792,128]{1,0:T(8,128)S(1)}) custom-call(bf16[256,12544]{1,0:T(8,128)(2,1)} %design.1, f32[256,128]{1,0:T(8,128)} %observed_in.1, s32[2,128]{1,0:T(2,128)} %bitcast.6, s32[1]{0:T(128)S(6)} %copy.9.counts, f32[1,128]{1,0:T(1,128)} %bitcast.7, f32[98,128]{1,0:T(8,128)} %bitcast.4, f32[98,128]{1,0:T(8,128)} %bitcast.5), custom_call_target="tpu_custom_call" | custom-call | tf_op jit(solution)/shard_map/pallas_call | solution.py:724
  183.6 1.3 constant_dynamic-slice_fusion
